TPU v7x, 256 devices: a whole 4x4x8 slice. The times are simulated.
256 devices in a mesh: outer: 4 (over x), inner: 64 (over z, y, core).
Axes of the slice: x: 4, y: 4, z: 8, core: 2. Of those that a mesh axis runs over, the one named last changes fastest.
Arguments:
- prim: float32 [8, 3072, 512], P(None, ('outer', 'inner')), may hold values from -4 to 9, as said below
- new_owner: int32 [3072], replicated, may hold values from 0 to 255, as said below
- new_slot: int32 [3072], replicated, may hold values from 0 to 23, as said below
Outputs:
- placed: float32 [8, 6144, 512], P(None, ('outer', 'inner'))
Inputs may be any that keep to these rules, and one draw needn't show every extreme that they name: `prim`: field 0 (density) lies in 0.3 to 3 and field 4 (pressure) in 0.2 to 9; fields 1 to 3 are velocities and 5 to 7 the magnetic field. `new_owner`: block g's owner lies in the segment of 64 devices that holds device g // 12 and differs from g // 12 by at most one; owners never fall along g, so every device gets a run of consecutive blocks (possibly none); at most 6 blocks of one device go to each neighbour, and in every draw some device of each segment receives 24 blocks. `new_slot`: the blocks of one owner have slots 0, 1, 2, ... in the order of g.
All inputs are finite; a program needn't handle non-finite values.
Results may differ from a plain program's by a relative error of at most 0.0003.
Values sent between devices are 32-bit elements; how exact they have to be, the bound alone decides.
No kernel may reach another device: no remote copies, remote signals or barrier semaphores. Data moves between devices by JAX's collectives and lax.ppermute only.
A program may use at most 64 MiB of HBM per device.

v0:
```python
import functools

import jax
import jax.numpy as jnp
from jax import lax
from jax.sharding import Mesh
from jax.sharding import PartitionSpec as P

BE = 8
GY = 16
OUTER_INNER = ("outer", "inner_0", "inner_1", "inner_2")
INNER = ("inner_0", "inner_1", "inner_2")


GAMMA = 5.0 / 3.0
COURANT = 0.8


def one_axis_at_a_time(value, axes):
    return functools.reduce(lax.pmax, axes, value)


def extended(value, sides, width):
    edges = {}
    for axis, dim in sides:
        count, length = (lax.axis_size(axis), value.shape[dim])
        up = [(i, (i + 1) % count) for i in range(count)]
        last = lax.slice_in_dim(value, length - width, length, axis=dim)
        first = lax.slice_in_dim(value, 0, width, axis=dim)
        edges[dim] = (
            lax.ppermute(last, axis, up),
            lax.ppermute(first, axis, [(b, a) for a, b in up]),
        )
    done = []
    for _, dim in sides:
        low, high = edges[dim]
        around = [(width, width) if d in done else (0, 0) for d in range(value.ndim)]
        value = jnp.concatenate([jnp.pad(low, around), value, jnp.pad(high, around)], axis=dim)
        done.append(dim)
    return value


def passed_along(value, axis, steps):
    count = lax.axis_size(axis)
    pairs = [(source, (source + steps) % count) for source in range(count)]
    return lax.ppermute(value, axis, pairs)


def shifted(value, axis, by):
    count = lax.axis_size(axis)
    pairs = [(i, i + by) for i in range(count) if 0 <= i + by < count]
    return lax.ppermute(value, axis, pairs)


def minmod(former, latter):
    return (
        0.5 * (jnp.sign(former) + jnp.sign(latter)) * jnp.minimum(jnp.abs(former), jnp.abs(latter))
    )


def unpack(state):
    return [state[component] for component in range(8)]


def conserved(state):
    density, speed_x, speed_y, speed_z, pressure, field_x, field_y, field_z = unpack(state)
    kinetic = 0.5 * density * (speed_x * speed_x + speed_y * speed_y + speed_z * speed_z)
    magnetic = 0.5 * (field_x * field_x + field_y * field_y + field_z * field_z)
    energy = pressure / (GAMMA - 1.0) + kinetic + magnetic
    return jnp.stack(
        [
            density,
            density * speed_x,
            density * speed_y,
            density * speed_z,
            energy,
            field_x,
            field_y,
            field_z,
        ]
    )


def signal(state):
    density, speed_x, speed_y, speed_z, pressure, field_x, field_y, field_z = unpack(state)
    field_sq = field_x * field_x + field_y * field_y + field_z * field_z
    return (
        jnp.abs(speed_x)
        + jnp.abs(speed_y)
        + jnp.abs(speed_z)
        + 3.0 * jnp.sqrt((GAMMA * pressure + field_sq) / density)
    )


def flux_parts(state, normal):
    density, speed_x, speed_y, speed_z, pressure, field_x, field_y, field_z = unpack(state)
    velocity = (speed_x, speed_y, speed_z)
    magnetic = (field_x, field_y, field_z)
    normal_speed = velocity[normal]
    normal_field = magnetic[normal]
    field_sq = field_x * field_x + field_y * field_y + field_z * field_z
    total_pressure = pressure + 0.5 * field_sq
    conserved_state = conserved(state)
    vel_dot_field = speed_x * field_x + speed_y * field_y + speed_z * field_z
    momentum = []
    for component in range(3):
        momentum_term = (
            density * velocity[component] * normal_speed - magnetic[component] * normal_field
        )
        if component == normal:
            momentum_term = momentum_term + total_pressure
        momentum.append(momentum_term)
    induction = [
        magnetic[component] * normal_speed - velocity[component] * normal_field
        for component in range(3)
    ]
    energy_flux = (
        conserved_state[4] + total_pressure
    ) * normal_speed - normal_field * vel_dot_field
    flux_terms = jnp.stack([density * normal_speed] + momentum + [energy_flux] + induction)
    signal_speed = jnp.abs(normal_speed) + jnp.sqrt((GAMMA * pressure + field_sq) / density)
    return (flux_terms, signal_speed, conserved_state)


def divergence(padded, normal):
    cell_axis = normal + 1
    inner_count = padded.shape[cell_axis] - 4

    def window(values, offset, length):
        return lax.slice_in_dim(values, offset, offset + length, axis=cell_axis)

    steps_between = window(padded, 1, inner_count + 3) - window(padded, 0, inner_count + 3)
    slopes = minmod(
        window(steps_between, 0, inner_count + 2), window(steps_between, 1, inner_count + 2)
    )
    centres = window(padded, 1, inner_count + 2)
    left_state = window(centres, 0, inner_count + 1) + 0.5 * window(slopes, 0, inner_count + 1)
    right_state = window(centres, 1, inner_count + 1) - 0.5 * window(slopes, 1, inner_count + 1)
    flux_left, speed_left, state_left = flux_parts(left_state, normal)
    flux_right, speed_right, state_right = flux_parts(right_state, normal)
    face_flux = 0.5 * (flux_left + flux_right) - 0.5 * jnp.maximum(speed_left, speed_right)[
        None
    ] * (state_right - state_left)
    return window(face_flux, 1, inner_count) - window(face_flux, 0, inner_count)


def advance(x_padded, y_padded, z_padded, time_step):
    middle = x_padded[:, 2:-2]
    change = divergence(x_padded, 0) + divergence(y_padded, 1) + divergence(z_padded, 2)
    return conserved(middle) - time_step * change


def split_blocks(values, blocks):
    leading, first_len, second_len, length = values.shape
    depth = length // blocks
    parted = values.reshape(leading, first_len, second_len, blocks, depth)
    return parted.transpose(0, 3, 1, 2, 4).reshape(leading, blocks, first_len * second_len * depth)


def place(candidates, new_owner, new_slot, device, blocks, reach):
    capacity = blocks + 2 * reach
    block_total = new_owner.shape[0]
    block_ids = device * blocks - reach + jnp.arange(capacity, dtype=jnp.int32)
    inside = (block_ids >= 0) & (block_ids < block_total)
    clipped = jnp.clip(block_ids, 0, block_total - 1)
    owned = inside & (new_owner[clipped] == device)
    slot_ids = jnp.arange(capacity, dtype=jnp.int32)
    chooser = (owned[None, :] & (new_slot[clipped][None, :] == slot_ids[:, None])).astype(
        jnp.float32
    )
    arrived = jnp.einsum("sc,fcx->fsx", chooser, candidates, precision=lax.Precision.HIGHEST)
    return (arrived, jnp.sum(chooser, axis=1))


def per_device(prim, new_owner, new_slot):
    blocks = prim.shape[1]
    edge_len = BE
    length = blocks * edge_len
    reach = blocks // 2
    pencil = (
        prim.reshape(8, blocks, edge_len, edge_len, edge_len)
        .transpose(0, 2, 3, 1, 4)
        .reshape(8, edge_len, edge_len, length)
    )
    fastest = one_axis_at_a_time(jnp.max(signal(pencil)), OUTER_INNER)
    time_step = COURANT / fastest
    device = lax.axis_index(OUTER_INNER)
    y_padded = extended(pencil, ((OUTER_INNER, 2),), 2)
    before_x = passed_along(pencil[:, edge_len - 2 :], OUTER_INNER, GY)
    after_x = passed_along(pencil[:, :2], OUTER_INNER, -GY)
    x_padded = jnp.concatenate([before_x, pencil, after_x], 1)
    z_padded = jnp.concatenate([pencil[..., -2:], pencil, pencil[..., :2]], 3)
    span = 4 * edge_len

    def advance_group(index):
        offset = index * span
        x_part = lax.dynamic_slice_in_dim(x_padded, offset, span, 3)
        y_part = lax.dynamic_slice_in_dim(y_padded, offset, span, 3)
        z_part = lax.dynamic_slice_in_dim(z_padded, offset, span + 4, 3)
        return advance(x_part, y_part, z_part, time_step)

    result = lax.map(advance_group, jnp.arange(blocks // 4, dtype=jnp.int32))
    result = result.transpose(1, 2, 3, 0, 4).reshape(8, edge_len, edge_len, length)
    updated = split_blocks(result, blocks)
    from_lower = shifted(updated[:, blocks - reach :], INNER, 1)
    from_upper = shifted(updated[:, :reach], INNER, -1)
    candidates = jnp.concatenate([from_lower, updated, from_upper], 1)
    arrived, live = place(candidates, new_owner, new_slot, device, blocks, reach)
    return arrived


def solution(mesh):
    split = Mesh(
        mesh.devices.reshape(mesh.shape["outer"], 8, 4, 2),
        ("outer", "inner_0", "inner_1", "inner_2"),
    )
    return jax.shard_map(
        per_device,
        mesh=split,
        in_specs=(P(None, OUTER_INNER, None), P(), P()),
        out_specs=P(None, OUTER_INNER, None),
        check_vma=False,
    )
```

profile of v0, /device:TPU:1, one launch (start us, length us, event | category | flops | bytes accessed | tf_op | source)
XLA Modules:
  0.0 109.6 jit_solution(17669402659921488361)
XLA Ops:
  0.0 2.7 %reshape.61 = f32[8,12,8,8,8]{4,3,2,0,1:T(8,128)S(1)} reshape(f32[8,12,512]{2,0,1:T(8,128)} %param.5) | data formatting | bytes 393216 | tf_op jit(solution)/shard_map/reshape | solution.py:181
  2.7 3.8 %copy.5 = f32[8,8,8,12,8]{4,3,2,1,0:T(8,128)} copy(f32[8,8,8,12,8]{4,2,1,0,3:T(8,128)S(1)} %bitcast.35) | data formatting | bytes 393216 | tf_op jit(solution)/shard_map/transpose | solution.py:182
  6.5 3.3 %reshape.62 = f32[8,8,8,96]{3,2,1,0:T(8,128)S(1)} reshape(f32[8,8,8,12,8]{4,3,2,1,0:T(8,128)} %copy.5) | data formatting | bytes 393216 | tf_op jit(solution)/shard_map/reshape | solution.py:183
  9.8 0.7 fusion.40
  10.5 2.7 %collective-permute-start.2 = (f32[8,8,2,96]{3,2,1,0:T(2,128)}, f32[8,8,2,96]{3,2,1,0:T(2,128)S(1)}, u32[]{:S(2)}, u32[]{:S(2)}) collective-permute-start(f32[8,8,2,96]{3,2,1,0:T(2,128)} %get-tuple-element.132), channel_id=1, source_target_pairs={{0,1},{1,2},{2,3},{3,4},{4,5},{5,6},{6,7},{7,8},{8,9},{9,10},{10,1... | collective-permute-start | bytes 147464 | tf_op jit(solution)/shard_map/ppermute | solution.py:31
  13.2 0.5 collective-permute-start.3
  13.7 0.7 fusion.41
  14.4 2.5 %collective-permute-start = (f32[8,2,8,96]{3,2,1,0:T(8,128)}, f32[8,2,8,96]{3,2,1,0:T(8,128)}, u32[]{:S(2)}, u32[]{:S(2)}) collective-permute-start(f32[8,2,8,96]{3,2,1,0:T(8,128)} %get-tuple-element.134), channel_id=1, source_target_pairs={{0,16},{1,17},{2,18},{3,19},{4,20},{5,21},{6,22},{7,23},{8,24},{9,... | collective-permute-start | bytes 147464 | tf_op jit(solution)/shard_map/ppermute | solution.py:46
  16.8 5.2 %collective-permute-start.1 = (f32[8,2,8,96]{3,2,1,0:T(8,128)}, f32[8,2,8,96]{3,2,1,0:T(8,128)}, u32[]{:S(2)}, u32[]{:S(2)}) collective-permute-start(f32[8,2,8,96]{3,2,1,0:T(8,128)} %get-tuple-element.135), channel_id=1, source_target_pairs={{0,240},{1,241},{2,242},{3,243},{4,244},{5,245},{6,246},{7,247},{8... | collective-permute-start | bytes 147464 | tf_op jit(solution)/shard_map/ppermute | solution.py:46
  22.1 1.0 fusion.30
  23.2 7.5 %pmax.28 = f32[]{:T(128)} all-reduce(f32[]{:T(128)} %fusion.30), channel_id=1, replica_groups=mesh['outer'=4,'inner_0'=8,'inner_1'=4,'inner_2'=2] {'outer'}, use_global_device_ids=true, to_apply=%region_1.0 | all-reduce | flops 1 | bytes 8 | tf_op jit(solution)/shard_map/pmax | solution.py:20
  30.7 12.6 %pmax.29 = f32[]{:T(128)} all-reduce(f32[]{:T(128)} %pmax.28), channel_id=1, replica_groups=mesh['outer'=4,'inner_0'=8,'inner_1'=4,'inner_2'=2] {'inner_0'}, use_global_device_ids=true, to_apply=%region_2.0 | all-reduce | flops 1 | bytes 8 | tf_op jit(solution)/shard_map/pmax | solution.py:20
  43.2 8.9 %pmax.30 = f32[]{:T(128)} all-reduce(f32[]{:T(128)} %pmax.29), channel_id=1, replica_groups=mesh['outer'=4,'inner_0'=8,'inner_1'=4,'inner_2'=2] {'inner_1'}, use_global_device_ids=true, to_apply=%region_3.0 | all-reduce | flops 1 | bytes 8 | tf_op jit(solution)/shard_map/pmax | solution.py:20
  52.3 12.2 %pmax.31 = f32[]{:T(128)} all-reduce(f32[]{:T(128)} %pmax.30), channel_id=1, replica_groups=mesh['outer'=4,'inner_0'=8,'inner_1'=4,'inner_2'=2] {'inner_2'}, use_global_device_ids=true, to_apply=%region_4.0 | all-reduce | flops 1 | bytes 8 | tf_op jit(solution)/shard_map/pmax | solution.py:20
  65.2 1.3 %gather_fusion = s32[24]{0:T(128)} fusion(s32[3072]{0:T(1024)S(1)} %copy-done, s32[1024]{0:T(1024)S(1)} %pad_clamp_fusion), kind=kCustom, calls=%fused_computation | custom fusion | bytes 288 | tf_op jit(solution)/shard_map/gather | solution.py:166
  66.6 0.9 pad_maximum_fusion.1
  67.6 21.3 %while.10 = (s32[]{:T(128)}, f32[3,8,8,8,32]{4,3,2,1,0:T(8,128)}, s32[3]{0:T(128)S(1)}, f32[8,12,8,96]{3,2,1,0:T(8,128)S(1)}, f32[]{:T(128)}, /*index=5*/f32[8,8...) while((s32[]{:T(128)}, f32[3,8,8,8,32]{4,3,2,1,0:T(8,128)}, ...), condition=%wide.region_6.7_spmd, body=%wide.region_5.6_spmd.sunk | while | flops 1960325 | bytes 22909688 | solution.py:202
  67.6 0.6 dynamic_slice.14
  73.8 0.9 fusion.49
  74.7 0.6 dynamic_slice.14
  80.9 0.8 fusion.49
  81.7 0.6 dynamic_slice.14
  88.0 0.8 fusion.49
  88.8 1.7 %copy.6 = f32[8,8,8,3,32]{4,3,2,1,0:T(4,128)S(1)} copy(f32[8,8,8,3,32]{4,2,1,0,3:T(8,128)} %bitcast.6) | data formatting | bytes 393216 | tf_op jit(solution)/shard_map/transpose | solution.py:203
  90.5 2.8 %reshape_reshape.3 = f32[8,8,8,12,8]{4,3,2,1,0:T(8,128)} reshape(f32[8,8,8,3,32]{4,3,2,1,0:T(4,128)S(1)} %copy.6) | data formatting | bytes 393216 | tf_op jit(solution)/shard_map/reshape;reshape | solution.py:156
  93.3 3.1 %copy.11 = f32[8,12,8,8,8]{4,3,2,1,0:T(8,128)S(1)} copy(f32[8,12,8,8,8]{4,1,3,2,0:T(8,128)} %bitcast.37) | data formatting | bytes 393216 | tf_op jit(solution)/shard_map/reshape | solution.py:157
  96.4 2.0 %reshape.81 = f32[8,12,512]{2,1,0:T(8,128)S(1)} reshape(f32[8,12,8,8,8]{4,3,2,1,0:T(8,128)S(1)} %copy.11) | data formatting | bytes 393216 | tf_op jit(solution)/shard_map/reshape | solution.py:157
  98.4 3.8 %collective-permute-start.4 = (f32[8,6,512]{2,1,0:T(8,128)S(1)}, f32[8,6,512]{2,1,0:T(8,128)S(1)}, u32[]{:S(2)}, u32[]{:S(2)}) collective-permute-start(f32[8,6,512]{2,1,0:T(8,128)S(1)} %get-tuple-element.128), channel_id=1, source_target_pairs={{0,1},{1,2},{2,3},{3,4},{4,5},{5,6},{6,7},{7,8},{8,9},{9,10},{10,1... | collective-permute-start | bytes 294920 | tf_op jit(solution)/shard_map/ppermute | solution.py:52
  102.2 1.9 %collective-permute-start.5 = (f32[8,6,512]{2,1,0:T(8,128)S(1)}, f32[8,6,512]{2,1,0:T(8,128)S(1)}, u32[]{:S(2)}, u32[]{:S(2)}) collective-permute-start(f32[8,6,512]{2,1,0:T(8,128)S(1)} %get-tuple-element.129), channel_id=1, source_target_pairs={{1,0},{2,1},{3,2},{4,3},{5,4},{6,5},{7,6},{8,7},{9,8},{10,9},{11,1... | collective-permute-start | bytes 294920 | tf_op jit(solution)/shard_map/ppermute | solution.py:52
  104.2 0.7 gather_fusion.1
  104.9 3.6 %collective-permute-done.5 = f32[8,6,512]{2,1,0:T(8,128)S(1)} collective-permute-done((f32[8,6,512]{2,1,0:T(8,128)S(1)}, f32[8,6,512]{2,1,0:T(8,128)S(1)}, u32[]{:S(2)}, u32[]{:S(2)}) %collective-permute-start.5) | collective-permute-done | bytes 98336 | tf_op jit(solution)/shard_map/ppermute | solution.py:52
  108.5 1.1 %convolution_bitcast_fusion = f32[8,24,512]{2,1,0:T(8,128)} fusion(f32[8,6,512]{2,1,0:T(8,128)S(1)} %collective-permute-done.5, f32[8,12,512]{2,1,0:T(8,128)S(1)} %reshape.81, f32[8,6,512]{2,1,0:T(8,128)S(1)} %collective-permute-done.4, s32[24]{0:T(128)S(1)} %gather_fusion.1, pred[24]{0:T(512)(128)(4,1)S(1)} %compare_and_fusion), kind=kOutput, calls=%fused_computation.176 | convolution fusion | flops 28509312 | bytes 786552 | tf_op jit(solution)/shard_map/sc,fcx->fsx/dot_general | solution.py:171
  (260 shorter events, 13.8 us)
Async XLA Ops:
  0.0 65.2 %copy-start = (s32[3072]{0:T(1024)S(1)}, s32[3072]{0:T(1024)}, u32[]{:S(2)}) copy-start(s32[3072]{0:T(1024)} %param.6) | copy-start | bytes 36868
  10.5 56.0 %collective-permute-start.2 = (f32[8,8,2,96]{3,2,1,0:T(2,128)}, f32[8,8,2,96]{3,2,1,0:T(2,128)S(1)}, u32[]{:S(2)}, u32[]{:S(2)}) collective-permute-start(f32[8,8,2,96]{3,2,1,0:T(2,128)} %get-tuple-element.132), channel_id=1, source_target_pairs={{0,1},{1,2},{2,3},{3,4},{4,5},{5,6},{6,7},{7,8},{8,9},{9,10},{10,1... | collective-permute-start | bytes 147464 | tf_op jit(solution)/shard_map/ppermute | solution.py:31
  13.2 53.3 %collective-permute-start.3 = (f32[8,8,2,96]{3,2,1,0:T(2,128)}, f32[8,8,2,96]{3,2,1,0:T(2,128)S(1)}, u32[]{:S(2)}, u32[]{:S(2)}) collective-permute-start(f32[8,8,2,96]{3,2,1,0:T(2,128)} %get-tuple-element.133), channel_id=1, source_target_pairs={{1,0},{2,1},{3,2},{4,3},{5,4},{6,5},{7,6},{8,7},{9,8},{10,9},{11,1... | collective-permute-start | bytes 147464 | tf_op jit(solution)/shard_map/ppermute | solution.py:32
  14.4 52.2 %collective-permute-start = (f32[8,2,8,96]{3,2,1,0:T(8,128)}, f32[8,2,8,96]{3,2,1,0:T(8,128)}, u32[]{:S(2)}, u32[]{:S(2)}) collective-permute-start(f32[8,2,8,96]{3,2,1,0:T(8,128)} %get-tuple-element.134), channel_id=1, source_target_pairs={{0,16},{1,17},{2,18},{3,19},{4,20},{5,21},{6,22},{7,23},{8,24},{9,... | collective-permute-start | bytes 147464 | tf_op jit(solution)/shard_map/ppermute | solution.py:46
  16.8 49.8 %collective-permute-start.1 = (f32[8,2,8,96]{3,2,1,0:T(8,128)}, f32[8,2,8,96]{3,2,1,0:T(8,128)}, u32[]{:S(2)}, u32[]{:S(2)}) collective-permute-start(f32[8,2,8,96]{3,2,1,0:T(8,128)} %get-tuple-element.135), channel_id=1, source_target_pairs={{0,240},{1,241},{2,242},{3,243},{4,244},{5,245},{6,246},{7,247},{8... | collective-permute-start | bytes 147464 | tf_op jit(solution)/shard_map/ppermute | solution.py:46
  96.4 7.8 %copy-start.2 = (s32[24]{0:T(128)S(1)}, s32[24]{0:T(128)}, u32[]{:S(2)}) copy-start(s32[24]{0:T(128)} %gather_fusion) | copy-start | bytes 292
  96.4 7.8 %copy-start.1 = (s32[3072]{0:T(1024)S(1)}, s32[3072]{0:T(1024)}, u32[]{:S(2)}) copy-start(s32[3072]{0:T(1024)} %param.7) | copy-start | bytes 36868
  98.4 6.5 %collective-permute-start.4 = (f32[8,6,512]{2,1,0:T(8,128)S(1)}, f32[8,6,512]{2,1,0:T(8,128)S(1)}, u32[]{:S(2)}, u32[]{:S(2)}) collective-permute-start(f32[8,6,512]{2,1,0:T(8,128)S(1)} %get-tuple-element.128), channel_id=1, source_target_pairs={{0,1},{1,2},{2,3},{3,4},{4,5},{5,6},{6,7},{7,8},{8,9},{9,10},{10,1... | collective-permute-start | bytes 294920 | tf_op jit(solution)/shard_map/ppermute | solution.py:52
  102.2 6.3 %collective-permute-start.5 = (f32[8,6,512]{2,1,0:T(8,128)S(1)}, f32[8,6,512]{2,1,0:T(8,128)S(1)}, u32[]{:S(2)}, u32[]{:S(2)}) collective-permute-start(f32[8,6,512]{2,1,0:T(8,128)S(1)} %get-tuple-element.129), channel_id=1, source_target_pairs={{1,0},{2,1},{3,2},{4,3},{5,4},{6,5},{7,6},{8,7},{9,8},{10,9},{11,1... | collective-permute-start | bytes 294920 | tf_op jit(solution)/shard_map/ppermute | solution.py:52
where the time goes:
time: 111 us; the launch traced here: 110 us
  blocking collectives  41.2 us (37%)
  local copies, waits for them, and re-layouts  25.4 us (23%)
  other arithmetic  17.2 us (15%)
  starting transfers between devices  16.6 us (15%)
  loops' own time  3.67 us (3%)
  waiting for transfers between devices  3.63 us (3%)
  matrix products  1.11 us (1%)
    pmax x4, blocking collectives, one_axis_at_a_time(): return functools.reduce(lax.pmax, axes, value)  41.2 us
    ppermute x2, starting transfers between devices, passed_along(): return lax.ppermute(value, axis, pairs)  7.69 us
    ppermute x2, starting transfers between devices, shifted(): return lax.ppermute(value, axis, pairs)  5.71 us
    reshape x2, local copies, waits for them, and re-layouts, split_blocks(): parted.transpose(0, 3, 1, 2, 4)  5.12 us
    transpose x1, local copies, waits for them, and re-layouts, per_device(): pencil = prim.reshape(8, blocks, edge_len, edge_len, edge_len).transpose(...  3.79 us
    another operation x1, loops' own time, per_device(): result = lax.map(advance_group, jnp.arange(blocks // 4, dtype=jnp.int32))  3.67 us
    ppermute x2, waiting for transfers between devices, shifted(): return lax.ppermute(value, axis, pairs)  3.62 us
    while x144, other arithmetic  3.56 us
  transfers between devices with their start and end apart: 6, of which 1 were waited for; matrix products, arithmetic and copies ran while one was open for 4% of the time, Pallas kernels for 0%

commit v1 on v0

v1 whole, which is shorter than its diff:
```python
import functools

import jax
import jax.numpy as jnp
from jax import lax
from jax.experimental import pallas as pl
from jax.experimental.pallas import tpu as pltpu
from jax.sharding import PartitionSpec as P

GY = 16
AXES = ("outer", "inner")
GAMMA = 5.0 / 3.0
COURANT = 0.8
LANES = 128
TILES = 4
FIELDS = 8
BLOCKS = 12
REACH = 6
CAP = 24


def roll(value, shift):
    return pltpu.roll(value, shift % LANES, 1)


def lane_ids(rows):
    return lax.broadcasted_iota(jnp.int32, (rows, LANES), 1)


def half_minmod(former, latter):
    return 0.5 * (
        jnp.maximum(jnp.minimum(former, latter), 0.0)
        + jnp.minimum(jnp.maximum(former, latter), 0.0)
    )


def sound(density, pressure, field_sq):
    pushed = GAMMA * pressure + field_sq
    return pushed * lax.rsqrt(pushed * density)


def squared(state):
    return state[5] * state[5] + state[6] * state[6] + state[7] * state[7]


def conserved(state, field_sq):
    density, pressure = state[0], state[4]
    momentum = [density * state[1 + k] for k in range(3)]
    kinetic = momentum[0] * state[1] + momentum[1] * state[2] + momentum[2] * state[3]
    energy = pressure * (1.0 / (GAMMA - 1.0)) + 0.5 * (kinetic + field_sq)
    return [density, *momentum, energy, state[5], state[6], state[7]]


def flux_parts(state, normal):
    field_sq = squared(state)
    total_pressure = state[4] + 0.5 * field_sq
    whole = conserved(state, field_sq)
    speed, field = state[1 + normal], state[5 + normal]
    along = state[1] * state[5] + state[2] * state[6] + state[3] * state[7]
    momentum = [whole[1 + k] * speed - state[5 + k] * field for k in range(3)]
    momentum[normal] = momentum[normal] + total_pressure
    induction = [
        None if k == normal else state[5 + k] * speed - state[1 + k] * field for k in range(3)
    ]
    energy = (whole[4] + total_pressure) * speed - field * along
    signal = jnp.abs(speed) + sound(state[0], state[4], field_sq)
    return [whole[1 + normal], *momentum, energy, *induction], signal, whole


def twice_face_flux(left, right, normal):
    flux_left, signal_left, whole_left = flux_parts(left, normal)
    flux_right, signal_right, whole_right = flux_parts(right, normal)
    fastest = jnp.maximum(signal_left, signal_right)
    result = []
    for k in range(FIELDS):
        spread = fastest * (whole_right[k] - whole_left[k])
        result.append(-spread if flux_left[k] is None else flux_left[k] + flux_right[k] - spread)
    return result


def cell_rows(tile, k, first=0, count=BLOCKS):
    return pl.ds((first * TILES + tile) * FIELDS + k, count, stride=TILES * FIELDS)


def device_index():
    return lax.axis_index(AXES[0]) * lax.axis_size(AXES[1]) + lax.axis_index(AXES[1])


def prepare_kernel(prim_ref, x_first_ref, x_second_ref, y_inner_ref, y_outer_ref, fastest_ref):
    device = device_index()
    odd_row = (device // GY) % 2 == 1
    odd = device % 2 == 1
    slot = (lane_ids(FIELDS) // 16) % TILES
    for block in range(BLOCKS):
        parts = [
            prim_ref[(block * TILES + tile) * FIELDS : (block * TILES + tile + 1) * FIELDS]
            for tile in range(TILES)
        ]
        low, high = parts[0], roll(parts[0], -48)
        for tile in range(1, TILES):
            low = jnp.where(slot == tile, roll(parts[tile], 16 * tile), low)
            high = jnp.where(slot == tile, roll(parts[tile], 16 * tile - 48), high)
        here = slice(block * FIELDS, (block + 1) * FIELDS)
        x_first_ref[here] = jnp.where(odd_row, parts[0], parts[-1])
        x_second_ref[here] = jnp.where(odd_row, parts[-1], parts[0])
        y_inner_ref[here] = jnp.where(odd, low, high)
        y_outer_ref[here] = jnp.where(odd, high, low)
    best = None
    for tile in range(TILES):
        state = [prim_ref[cell_rows(tile, k)] for k in range(FIELDS)]
        speed = (
            jnp.abs(state[1])
            + jnp.abs(state[2])
            + jnp.abs(state[3])
            + 3.0 * sound(state[0], state[4], squared(state))
        )
        best = speed if best is None else jnp.maximum(best, speed)
    fastest_ref[...] = jnp.broadcast_to(jnp.max(best, keepdims=True), fastest_ref.shape)


def change_kernel(
    prim_ref, x_first_ref, x_second_ref, y_inner_ref, y_outer_ref, own_ref, inner_ref, outer_ref
):
    device = device_index()
    odd_row = (device // GY) % 2 == 1
    odd = device % 2 == 1
    lane = lane_ids(BLOCKS)
    first_half = lane < 64
    y_low = (lane % 64) < 8
    y_high = (lane % 64) >= 56
    z_low = (lane % 8) == 0
    z_high = (lane % 8) == 7
    packed_slot = (lane // 16) % TILES

    def either(first, second, k, flag):
        rows = pl.ds(k, BLOCKS, stride=FIELDS)
        return jnp.where(flag, first[rows], second[rows])

    fields = range(FIELDS)
    cells = [[prim_ref[cell_rows(tile, k)] for k in fields] for tile in range(TILES)]
    total = [[None] * FIELDS for _ in range(TILES)]

    before = [either(x_first_ref, x_second_ref, k, odd_row) for k in fields]
    after = [either(x_second_ref, x_first_ref, k, odd_row) for k in fields]
    line = [before] + cells + [after]
    turned = [[roll(value, 64) for value in part] for part in line]
    lefts, rights = [], []
    for tile in range(TILES + 2):
        left, right = [], []
        for k in fields:
            here = line[tile][k]
            down = turned[max(tile - 1, 0)][k]
            up = turned[min(tile + 1, TILES + 1)][k]
            same = turned[tile][k]
            half = half_minmod(
                here - jnp.where(first_half, down, same), jnp.where(first_half, same, up) - here
            )
            left.append(here + half)
            right.append(roll(here - half, 64))
        lefts.append(left)
        rights.append(right)
    previous = None
    for tile in range(TILES + 1):
        right = [jnp.where(first_half, rights[tile][k], rights[tile + 1][k]) for k in fields]
        face = twice_face_flux(lefts[tile], right, 0)
        turned_face = [roll(value, 64) for value in face]
        if tile > 0:
            for k in fields:
                total[tile - 1][k] = face[k] - jnp.where(
                    first_half, previous[k], turned_face[k]
                )
        previous = turned_face

    low_halo = [either(y_inner_ref, y_outer_ref, k, odd) for k in fields]
    high_halo = [either(y_outer_ref, y_inner_ref, k, odd) for k in fields]
    low_left, low_right, high_right = [], [], []
    for k in fields:
        low, high = cells[0][k], roll(cells[0][k], -48)
        for tile in range(1, TILES):
            low = jnp.where(packed_slot == tile, roll(cells[tile][k], 16 * tile), low)
            high = jnp.where(packed_slot == tile, roll(cells[tile][k], 16 * tile - 48), high)
        outside, edge = low_halo[k], roll(low, 8)
        step = edge - outside
        low_left.append(outside + half_minmod(outside - roll(outside, 8), step))
        low_right.append(edge - half_minmod(step, low - edge))
        outside = high_halo[k]
        high_right.append(
            outside - half_minmod(outside - roll(high, -8), roll(outside, -8) - outside)
        )
    low_face = twice_face_flux(low_left, low_right, 1)
    for tile in range(TILES):
        to_low, to_high = -8 * (2 * tile + 1), 8 * (7 - 2 * tile)
        left, right = [], []
        for k in fields:
            here = cells[tile][k]
            down = jnp.where(y_low, roll(low_halo[k], to_low), roll(here, 8))
            up = jnp.where(y_high, roll(high_halo[k], to_high), roll(here, -8))
            half = half_minmod(here - down, up - here)
            left.append(here + half)
            right.append(
                jnp.where(y_high, roll(high_right[k], to_high), roll(here - half, -8))
            )
        face = twice_face_flux(left, right, 1)
        for k in fields:
            down = jnp.where(y_low, roll(low_face[k], to_low), roll(face[k], 8))
            total[tile][k] = total[tile][k] + (face[k] - down)

    def next_cell(value):
        turned = roll(value, 7)
        turned = jnp.concatenate([turned[1:], turned[:1]], 0)
        return jnp.where(z_high, turned, roll(value, -1))

    def last_cell(value):
        turned = roll(value, -7)
        turned = jnp.concatenate([turned[-1:], turned[:-1]], 0)
        return jnp.where(z_low, turned, roll(value, 1))

    for tile in range(TILES):
        left, right = [], []
        for k in fields:
            here = cells[tile][k]
            half = half_minmod(here - last_cell(here), next_cell(here) - here)
            left.append(here + half)
            right.append(next_cell(here - half))
        face = twice_face_flux(left, right, 2)
        whole = conserved(cells[tile], squared(cells[tile]))
        for k in fields:
            change = total[tile][k] + (face[k] - last_cell(face[k]))
            own_ref.at[0][cell_rows(tile, k)] = whole[k]
            own_ref.at[1][cell_rows(tile, k)] = change

    half = REACH * TILES * FIELDS
    to_inner = pl.multiple_of(jnp.where(odd, 0, half), FIELDS)
    to_outer = pl.multiple_of(jnp.where(odd, half, 0), FIELDS)
    for part in range(2):
        inner_ref[part] = own_ref[part, pl.ds(to_inner, half)]
        outer_ref[part] = own_ref[part, pl.ds(to_outer, half)]


def place_kernel(fastest_ref, own_ref, inner_ref, outer_ref, owner_ref, out_ref, held_ref):
    device = device_index()
    odd = device % 2 == 1
    scale = (0.5 * COURANT) / jnp.max(fastest_ref[...])
    half = REACH * TILES * FIELDS

    def stepped(ref):
        return ref[0] - scale * ref[1]

    inner, outer = stepped(inner_ref), stepped(outer_ref)
    held_ref[:half] = jnp.where(odd, inner, outer)
    held_ref[half : 3 * half] = stepped(own_ref)
    held_ref[3 * half : 4 * half] = jnp.where(odd, outer, inner)
    owners = owner_ref[...]
    first = jnp.sum((owners < device).astype(jnp.int32)) - (device * BLOCKS - REACH)
    count = jnp.sum((owners == device).astype(jnp.int32))
    first = jnp.clip(first, 0, BLOCKS)
    live = lax.broadcasted_iota(jnp.int32, (CAP, LANES), 0) < count
    for k in range(FIELDS):
        for tile in range(TILES):
            value = held_ref[cell_rows(tile, k, first, CAP)]
            out_ref[k, :, tile * LANES : (tile + 1) * LANES] = jnp.where(live, value, 0.0)


def call(kernel, outs, name, flops, scratch=()):
    return pl.pallas_call(
        kernel,
        out_shape=[jax.ShapeDtypeStruct(shape, jnp.float32) for shape in outs],
        scratch_shapes=list(scratch),
        cost_estimate=pl.CostEstimate(flops=flops, bytes_accessed=flops // 8, transcendentals=0),
        name=name,
    )


def swap(value, partner, devices):
    pairs = [(i, partner(i) % devices) for i in range(devices) if partner(i) is not None]
    return lax.ppermute(value, AXES, pairs)


def per_device(ranks, prim, new_owner, new_slot):
    del new_slot
    devices = lax.axis_size(AXES)
    rows = BLOCKS * TILES * FIELDS
    raw = prim.reshape(FIELDS, BLOCKS, TILES, LANES).transpose(1, 2, 0, 3).reshape(rows, LANES)
    side = (BLOCKS * FIELDS, LANES)
    x_first, x_second, y_inner, y_outer, fastest = call(
        prepare_kernel, [side, side, side, side, (devices, LANES)], "prepare", 10**6
    )(raw)
    everyone = lax.all_to_all(fastest, AXES, 0, 0, tiled=True)

    def within(i, j):
        return j if 0 <= j < devices and i // ranks == j // ranks else None

    x_first = swap(x_first, lambda i: i + GY if (i // GY) % 2 == 0 else i - GY, devices)
    x_second = swap(x_second, lambda i: i + GY if (i // GY) % 2 == 1 else i - GY, devices)
    y_outer = swap(y_outer, lambda i: i + 1 if i % 2 == 1 else i - 1, devices)
    y_inner = swap(y_inner, lambda i: i ^ 1, devices)
    half = (2, rows // 2, LANES)
    own, to_inner, to_outer = call(
        change_kernel, [(2, rows, LANES), half, half], "change", 2 * 10**7
    )(raw, x_first, x_second, y_inner, y_outer)
    from_outer = swap(to_outer, lambda i: within(i, i + 1 if i % 2 == 1 else i - 1), devices)
    from_inner = swap(to_inner, lambda i: i ^ 1, devices)
    (placed,) = call(
        place_kernel,
        [(FIELDS, CAP, TILES * LANES)],
        "place",
        10**6,
        [pltpu.VMEM((3 * rows, LANES), jnp.float32)],
    )(everyone, own, from_inner, from_outer, new_owner.reshape(-1, LANES))
    return placed


def solution(mesh):
    return jax.shard_map(
        functools.partial(per_device, mesh.shape["inner"]),
        mesh=mesh,
        in_specs=(P(None, AXES, None), P(), P()),
        out_specs=P(None, AXES, None),
        check_vma=False,
    )
```

time: 111 us -> 56.5 us (0.51); the launches traced: 110 us -> 56.3 us
  blocking collectives: 41.2 us -> 0 us
  local copies, waits for them, and re-layouts: 25.4 us -> 1.37 us
  starting transfers between devices: 16.6 us -> 34 us
  other arithmetic: 17.2 us -> 0 us
  Pallas kernels: 0 us -> 13.3 us
  waiting for transfers between devices: 3.63 us -> 7.54 us
  loops' own time: 3.67 us -> 0 us
  matrix products: 1.11 us -> 0 us
    pmax x4 -> x0, blocking collectives: 41.2 us -> none  [one_axis_at_a_time(): return functools.reduce(lax.pmax, axes, value)]
    all_to_all x0 -> x1, starting transfers between devices: none -> 15.7 us  [per_device(): everyone = lax.all_to_all(fastest, AXES, 0, 0, tiled=True)]
    pallas_call x0 -> x3, Pallas kernels: none -> 13.3 us  [the longest x1 9.01 us: per_device(): call(change_kernel, [(2, rows, LANES), half, half], 'change', 2 * 10 ** 7)]
    reshape x4 -> x0, local copies, waits for them, and re-layouts: 11.1 us -> none  [the longest x2 5.12 us: split_blocks(): parted.transpose(0, 3, 1, 2, 4)]
    transpose x2 -> x0, local copies, waits for them, and re-layouts: 5.46 us -> none  [the longest x1 3.79 us: per_device(): pencil = prim.reshape(8, blocks, edge_len, edge_len, edge_len).transpose(...]
    ppermute x6, waiting for transfers between devices: 3.63 us -> 7.53 us  [swap(): return lax.ppermute(value, AXES, pairs)]
    another operation x1 -> x0, loops' own time: 3.67 us -> none  [per_device(): result = lax.map(advance_group, jnp.arange(blocks // 4, dtype=jnp.int32))]
    while x144 -> x0, other arithmetic: 3.56 us -> none
  transfers between devices with their start and end apart: 6 -> 7, of which waited for: 1 -> 3; matrix products, arithmetic and copies ran while one was open for 4% -> 0% of each run, Pallas kernels for 0% -> 16%
where the time goes in v1:
time: 56.5 us; the launch traced here: 56.3 us
  starting transfers between devices  34 us (60%)
  Pallas kernels  13.3 us (24%)
  waiting for transfers between devices  7.54 us (13%)
  local copies, waits for them, and re-layouts  1.37 us (2%)
    ppermute x6, starting transfers between devices, swap(): return lax.ppermute(value, AXES, pairs)  18.3 us
    all_to_all x1, starting transfers between devices, per_device(): everyone = lax.all_to_all(fastest, AXES, 0, 0, tiled=True)  15.7 us
    pallas_call x1, Pallas kernels, per_device(): call(change_kernel, [(2, rows, LANES), half, half], 'change', 2 * 10 ** 7)  9.01 us
    ppermute x6, waiting for transfers between devices, swap(): return lax.ppermute(value, AXES, pairs)  7.53 us
    pallas_call x1, Pallas kernels, per_device(): call(place_kernel, [(FIELDS, CAP, TILES * LANES)], 'place', 10 ** 6, [plt...  2.4 us
    pallas_call x1, Pallas kernels, per_device(): call(prepare_kernel, [side, side, side, side, (devices, LANES)], 'prepare...  1.88 us
    unnamed x22, local copies, waits for them, and re-layouts  1.37 us
  transfers between devices with their start and end apart: 7, of which 3 were waited for; matrix products, arithmetic and copies ran while one was open for 0% of the time, Pallas kernels for 16%

profile of v1, /device:TPU:1, one launch (start us, length us, event | category | flops | bytes accessed | tf_op | source)
XLA Modules:
  0.0 56.3 jit_solution(15316806251821252636)
XLA Ops:
  0.0 1.9 %prepare.1 = (f32[96,128]{1,0:T(8,128)}, f32[96,128]{1,0:T(8,128)}, f32[96,128]{1,0:T(8,128)}, f32[96,128]{1,0:T(8,128)}, f32[256,128]{1,0:T(8,128)}) custom-call(f32[384,128]{1,0:T(8,128)} %bitcast.10), custom_call_target="tpu_custom_call" | custom-call | flops 1000000 | bytes 125000 | tf_op jit(solution)/shard_map/prepare/pallas_call | solution.py:285
  1.9 0.0 copy-start.10
  1.9 0.0 copy-start.9
  1.9 15.7 %all-to-all-start = ((f32[256,1,128]{2,1,0:T(1,128)}), f32[256,1,128]{2,1,0:T(1,128)S(1)}, u32[]{:S(2)}, u32[]{:S(2)}) async-start(f32[256,1,128]{2,1,0:T(1,128)} %bitcast.13), calls=%async_computation | async-start | bytes 262144 | tf_op jit(solution)/shard_map/all_to_all | solution.py:288
  17.6 0.0 copy-done.10
  17.6 2.7 %collective-permute-start = (f32[96,128]{1,0:T(8,128)S(1)}, f32[96,128]{1,0:T(8,128)S(1)}, u32[]{:S(2)}, u32[]{:S(2)}) collective-permute-start(f32[96,128]{1,0:T(8,128)S(1)} %copy-done.10), channel_id=1, source_target_pairs={{0,16},{1,17},{2,18},{3,19},{4,20},{5,21},{6,22},{7,23},{8,24},{9,... | collective-permute-start | bytes 147464 | tf_op jit(solution)/shard_map/ppermute | solution.py:276
  20.3 0.0 copy-done.9
  20.3 6.0 %collective-permute-start.1 = (f32[96,128]{1,0:T(8,128)S(1)}, f32[96,128]{1,0:T(8,128)S(1)}, u32[]{:S(2)}, u32[]{:S(2)}) collective-permute-start(f32[96,128]{1,0:T(8,128)S(1)} %copy-done.9), channel_id=1, source_target_pairs={{0,240},{1,241},{2,242},{3,243},{4,244},{5,245},{6,246},{7,247},{8... | collective-permute-start | bytes 147464 | tf_op jit(solution)/shard_map/ppermute | solution.py:276
  26.3 0.0 copy-done.8
  26.3 0.9 %collective-permute-start.2 = (f32[96,128]{1,0:T(8,128)S(1)}, f32[96,128]{1,0:T(8,128)S(1)}, u32[]{:S(2)}, u32[]{:S(2)}) collective-permute-start(f32[96,128]{1,0:T(8,128)S(1)} %copy-done.8), channel_id=1, source_target_pairs={{0,1},{1,0},{2,3},{3,2},{4,5},{5,4},{6,7},{7,6},{8,9},{9,8},{10,11... | collective-permute-start | bytes 147464 | tf_op jit(solution)/shard_map/ppermute | solution.py:276
  27.2 0.0 copy-done.7
  27.2 1.2 %collective-permute-start.3 = (f32[96,128]{1,0:T(8,128)S(1)}, f32[96,128]{1,0:T(8,128)S(1)}, u32[]{:S(2)}, u32[]{:S(2)}) collective-permute-start(f32[96,128]{1,0:T(8,128)S(1)} %copy-done.7), channel_id=1, source_target_pairs={{0,255},{1,2},{2,1},{3,4},{4,3},{5,6},{6,5},{7,8},{8,7},{9,10},{10... | collective-permute-start | bytes 147464 | tf_op jit(solution)/shard_map/ppermute | solution.py:276
  28.5 0.0 collective-permute-done.x_first_ref
  28.5 0.1 collective-permute-done.1.x_second_ref
  28.6 0.0 collective-permute-done.2.y_inner_ref
  28.6 2.1 %collective-permute-done.3.y_outer_ref = f32[96,128]{1,0:T(8,128)S(1)} collective-permute-done((f32[96,128]{1,0:T(8,128)S(1)}, f32[96,128]{1,0:T(8,128)S(1)}, u32[]{:S(2)}, u32[]{:S(2)}) %collective-permute-start.3) | collective-permute-done | bytes 49184 | tf_op jit(solution)/shard_map/ppermute | solution.py:276
  30.8 0.0 copy-done.3
  30.8 0.0 copy-done.4
  30.8 0.0 copy-done.5
  30.8 0.0 copy-start.6
  30.8 0.6 %copy-done.6 = f32[96,128]{1,0:T(8,128)} copy-done((f32[96,128]{1,0:T(8,128)}, f32[96,128]{1,0:T(8,128)S(1)}, u32[]{:S(2)}) %copy-start.6) | copy-done | bytes 49176
  31.4 9.0 %change.1 = (f32[2,384,128]{2,1,0:T(8,128)}, f32[2,192,128]{2,1,0:T(8,128)}, f32[2,192,128]{2,1,0:T(8,128)}) custom-call(f32[384,128]{1,0:T(8,128)} %bitcast.11, f32[96,128]{1,0:T(8,128)} %copy-done.3, f32[96,128]{1,0:T(8,128)} %copy-done.4, f32[96,128]{1,0:T(8,128)} %copy-done.5, f32[96,128]{1,0:T(8,128)} %copy-done.6), custom_call_target="tpu_custom_call" | custom-call | flops 20000000 | bytes 2500000 | tf_op jit(solution)/shard_map/change/pallas_call | solution.py:298
  40.4 5.5 %collective-permute-start.4 = (f32[2,192,128]{2,1,0:T(8,128)}, f32[2,192,128]{2,1,0:T(8,128)S(1)}, u32[]{:S(2)}, u32[]{:S(2)}) collective-permute-start(f32[2,192,128]{2,1,0:T(8,128)} %get-tuple-element.19), channel_id=1, source_target_pairs={{0,1},{1,0},{2,3},{3,2},{4,5},{5,4},{6,7},{7,6},{8,9},{9,8},{10,11... | collective-permute-start | bytes 589832 | tf_op jit(solution)/shard_map/ppermute | solution.py:276
  45.9 1.9 %collective-permute-start.5 = (f32[2,192,128]{2,1,0:T(8,128)}, f32[2,192,128]{2,1,0:T(8,128)S(1)}, u32[]{:S(2)}, u32[]{:S(2)}) collective-permute-start(f32[2,192,128]{2,1,0:T(8,128)} %get-tuple-element.20), channel_id=1, source_target_pairs={{1,2},{2,1},{3,4},{4,3},{5,6},{6,5},{7,8},{8,7},{9,10},{10,9},{11,... | collective-permute-start | bytes 589832 | tf_op jit(solution)/shard_map/ppermute | solution.py:276
  47.9 0.0 collective-permute-done.4.inner_ref
  47.9 0.0 copy-start.1
  47.9 5.3 %collective-permute-done.5.outer_ref = f32[2,192,128]{2,1,0:T(8,128)S(1)} collective-permute-done((f32[2,192,128]{2,1,0:T(8,128)}, f32[2,192,128]{2,1,0:T(8,128)S(1)}, u32[]{:S(2)}, u32[]{:S(2)}) %collective-permute-start.5) | collective-permute-done | bytes 196640 | tf_op jit(solution)/shard_map/ppermute | solution.py:276
  53.1 0.0 all-to-all-done
  53.1 0.0 copy-done.1
  53.1 0.7 %copy-done.2 = f32[2,192,128]{2,1,0:T(8,128)} copy-done((f32[2,192,128]{2,1,0:T(8,128)}, f32[2,192,128]{2,1,0:T(8,128)S(1)}, u32[]{:S(2)}) %copy-start.2) | copy-done | bytes 196632
  53.8 0.0 copy-done
  53.9 2.4 %place.1 = f32[8,24,512]{2,1,0:T(8,128)} custom-call(f32[256,128]{1,0:T(8,128)} %bitcast.12, f32[2,384,128]{2,1,0:T(8,128)} %get-tuple-element.18.own_ref, f32[2,192,128]{2,1,0:T(8,128)} %copy-done.1, f32[2,192,128]{2,1,0:T(8,128)} %copy-done.2, s32[24,128]{1,0:T(8,128)} %bitcast.14), custom_call_target="tpu_custom_call" | custom-call | flops 1000000 | bytes 125000 | tf_op jit(solution)/shard_map/place/pallas_call | solution.py:303
  (7 shorter events, 0.0 us)
Async XLA Ops:
  1.9 15.7 %copy-start.10 = (f32[96,128]{1,0:T(8,128)S(1)}, f32[96,128]{1,0:T(8,128)}, u32[]{:S(2)}) copy-start(f32[96,128]{1,0:T(8,128)} %get-tuple-element.14) | copy-start | bytes 147460
  1.9 18.4 %copy-start.9 = (f32[96,128]{1,0:T(8,128)S(1)}, f32[96,128]{1,0:T(8,128)}, u32[]{:S(2)}) copy-start(f32[96,128]{1,0:T(8,128)} %get-tuple-element.15) | copy-start | bytes 147460
  1.9 24.4 %copy-start.8 = (f32[96,128]{1,0:T(8,128)S(1)}, f32[96,128]{1,0:T(8,128)}, u32[]{:S(2)}) copy-start(f32[96,128]{1,0:T(8,128)} %get-tuple-element.16) | copy-start | bytes 147460
  1.9 25.4 %copy-start.7 = (f32[96,128]{1,0:T(8,128)S(1)}, f32[96,128]{1,0:T(8,128)}, u32[]{:S(2)}) copy-start(f32[96,128]{1,0:T(8,128)} %get-tuple-element.17) | copy-start | bytes 147460
  1.9 51.2 %all-to-all-start = ((f32[256,1,128]{2,1,0:T(1,128)}), f32[256,1,128]{2,1,0:T(1,128)S(1)}, u32[]{:S(2)}, u32[]{:S(2)}) async-start(f32[256,1,128]{2,1,0:T(1,128)} %bitcast.13), calls=%async_computation | async-start | bytes 262144 | tf_op jit(solution)/shard_map/all_to_all | solution.py:288
  17.6 10.9 %collective-permute-start = (f32[96,128]{1,0:T(8,128)S(1)}, f32[96,128]{1,0:T(8,128)S(1)}, u32[]{:S(2)}, u32[]{:S(2)}) collective-permute-start(f32[96,128]{1,0:T(8,128)S(1)} %copy-done.10), channel_id=1, source_target_pairs={{0,16},{1,17},{2,18},{3,19},{4,20},{5,21},{6,22},{7,23},{8,24},{9,... | collective-permute-start | bytes 147464 | tf_op jit(solution)/shard_map/ppermute | solution.py:276
  20.3 8.3 %collective-permute-start.1 = (f32[96,128]{1,0:T(8,128)S(1)}, f32[96,128]{1,0:T(8,128)S(1)}, u32[]{:S(2)}, u32[]{:S(2)}) collective-permute-start(f32[96,128]{1,0:T(8,128)S(1)} %copy-done.9), channel_id=1, source_target_pairs={{0,240},{1,241},{2,242},{3,243},{4,244},{5,245},{6,246},{7,247},{8... | collective-permute-start | bytes 147464 | tf_op jit(solution)/shard_map/ppermute | solution.py:276
  26.3 2.3 %collective-permute-start.2 = (f32[96,128]{1,0:T(8,128)S(1)}, f32[96,128]{1,0:T(8,128)S(1)}, u32[]{:S(2)}, u32[]{:S(2)}) collective-permute-start(f32[96,128]{1,0:T(8,128)S(1)} %copy-done.8), channel_id=1, source_target_pairs={{0,1},{1,0},{2,3},{3,2},{4,5},{5,4},{6,7},{7,6},{8,9},{9,8},{10,11... | collective-permute-start | bytes 147464 | tf_op jit(solution)/shard_map/ppermute | solution.py:276
  27.2 3.5 %collective-permute-start.3 = (f32[96,128]{1,0:T(8,128)S(1)}, f32[96,128]{1,0:T(8,128)S(1)}, u32[]{:S(2)}, u32[]{:S(2)}) collective-permute-start(f32[96,128]{1,0:T(8,128)S(1)} %copy-done.7), channel_id=1, source_target_pairs={{0,255},{1,2},{2,1},{3,4},{4,3},{5,6},{6,5},{7,8},{8,7},{9,10},{10... | collective-permute-start | bytes 147464 | tf_op jit(solution)/shard_map/ppermute | solution.py:276
  28.5 2.3 %copy-start.3 = (f32[96,128]{1,0:T(8,128)}, f32[96,128]{1,0:T(8,128)S(1)}, u32[]{:S(2)}) copy-start(f32[96,128]{1,0:T(8,128)S(1)} %collective-permute-done.x_first_ref) | copy-start | bytes 147460
  28.6 2.1 %copy-start.4 = (f32[96,128]{1,0:T(8,128)}, f32[96,128]{1,0:T(8,128)S(1)}, u32[]{:S(2)}) copy-start(f32[96,128]{1,0:T(8,128)S(1)} %collective-permute-done.1.x_second_ref) | copy-start | bytes 147460
  28.6 2.1 %copy-start.5 = (f32[96,128]{1,0:T(8,128)}, f32[96,128]{1,0:T(8,128)S(1)}, u32[]{:S(2)}) copy-start(f32[96,128]{1,0:T(8,128)S(1)} %collective-permute-done.2.y_inner_ref) | copy-start | bytes 147460
  30.8 0.6 %copy-start.6 = (f32[96,128]{1,0:T(8,128)}, f32[96,128]{1,0:T(8,128)S(1)}, u32[]{:S(2)}) copy-start(f32[96,128]{1,0:T(8,128)S(1)} %collective-permute-done.3.y_outer_ref) | copy-start | bytes 147460
  40.4 7.5 %collective-permute-start.4 = (f32[2,192,128]{2,1,0:T(8,128)}, f32[2,192,128]{2,1,0:T(8,128)S(1)}, u32[]{:S(2)}, u32[]{:S(2)}) collective-permute-start(f32[2,192,128]{2,1,0:T(8,128)} %get-tuple-element.19), channel_id=1, source_target_pairs={{0,1},{1,0},{2,3},{3,2},{4,5},{5,4},{6,7},{7,6},{8,9},{9,8},{10,11... | collective-permute-start | bytes 589832 | tf_op jit(solution)/shard_map/ppermute | solution.py:276
  45.9 7.2 %collective-permute-start.5 = (f32[2,192,128]{2,1,0:T(8,128)}, f32[2,192,128]{2,1,0:T(8,128)S(1)}, u32[]{:S(2)}, u32[]{:S(2)}) collective-permute-start(f32[2,192,128]{2,1,0:T(8,128)} %get-tuple-element.20), channel_id=1, source_target_pairs={{1,2},{2,1},{3,4},{4,3},{5,6},{6,5},{7,8},{8,7},{9,10},{10,9},{11,... | collective-permute-start | bytes 589832 | tf_op jit(solution)/shard_map/ppermute | solution.py:276
  47.9 5.3 %copy-start.1 = (f32[2,192,128]{2,1,0:T(8,128)}, f32[2,192,128]{2,1,0:T(8,128)S(1)}, u32[]{:S(2)}) copy-start(f32[2,192,128]{2,1,0:T(8,128)S(1)} %collective-permute-done.4.inner_ref) | copy-start | bytes 589828
  53.1 0.7 %copy-start.2 = (f32[2,192,128]{2,1,0:T(8,128)}, f32[2,192,128]{2,1,0:T(8,128)S(1)}, u32[]{:S(2)}) copy-start(f32[2,192,128]{2,1,0:T(8,128)S(1)} %collective-permute-done.5.outer_ref) | copy-start | bytes 589828
  53.1 0.7 %copy-start = (f32[256,1,128]{2,1,0:T(1,128)}, f32[256,1,128]{2,1,0:T(1,128)S(1)}, u32[]{:S(2)}) copy-start(f32[256,1,128]{2,1,0:T(1,128)S(1)} %all-to-all-done) | copy-start | bytes 393220

commit v2 on v1

--- a/solution.py
+++ b/solution.py
@@ -6,6 +6,7 @@
 from jax.experimental import pallas as pl
 from jax.experimental.pallas import tpu as pltpu
 from jax.sharding import PartitionSpec as P
+
 
 GY = 16
 AXES = ("outer", "inner")
@@ -261,13 +262,13 @@
             out_ref[k, :, tile * LANES : (tile + 1) * LANES] = jnp.where(live, value, 0.0)
 
 
-def call(kernel, outs, name, flops, scratch=()):
+def call(kernel, outs, flops, scratch=()):
     return pl.pallas_call(
         kernel,
         out_shape=[jax.ShapeDtypeStruct(shape, jnp.float32) for shape in outs],
         scratch_shapes=list(scratch),
         cost_estimate=pl.CostEstimate(flops=flops, bytes_accessed=flops // 8, transcendentals=0),
-        name=name,
+        compiler_params=pltpu.CompilerParams(vmem_limit_bytes=8 * 2**20),
     )
 
 
@@ -283,7 +284,7 @@
     raw = prim.reshape(FIELDS, BLOCKS, TILES, LANES).transpose(1, 2, 0, 3).reshape(rows, LANES)
     side = (BLOCKS * FIELDS, LANES)
     x_first, x_second, y_inner, y_outer, fastest = call(
-        prepare_kernel, [side, side, side, side, (devices, LANES)], "prepare", 10**6
+        prepare_kernel, [side, side, side, side, (devices, LANES)], 10**6
     )(raw)
     everyone = lax.all_to_all(fastest, AXES, 0, 0, tiled=True)
 
@@ -296,14 +297,13 @@
     y_inner = swap(y_inner, lambda i: i ^ 1, devices)
     half = (2, rows // 2, LANES)
     own, to_inner, to_outer = call(
-        change_kernel, [(2, rows, LANES), half, half], "change", 2 * 10**7
+        change_kernel, [(2, rows, LANES), half, half], 2 * 10**7
     )(raw, x_first, x_second, y_inner, y_outer)
     from_outer = swap(to_outer, lambda i: within(i, i + 1 if i % 2 == 1 else i - 1), devices)
     from_inner = swap(to_inner, lambda i: i ^ 1, devices)
     (placed,) = call(
         place_kernel,
         [(FIELDS, CAP, TILES * LANES)],
-        "place",
         10**6,
         [pltpu.VMEM((3 * rows, LANES), jnp.float32)],
     )(everyone, own, from_inner, from_outer, new_owner.reshape(-1, LANES))

time: 56.5 us -> 51.7 us (0.915)
  Pallas kernels: 13.3 us -> 9.3 us
    pallas_call x3, Pallas kernels: 13.3 us -> 9.3 us  [the longest x1 7.16 us: per_device(): call(change_kernel, [(2, rows, LANES), half, half], 2 * 10 ** 7)]
    unnamed x22 -> x6, local copies, waits for them, and re-layouts: 1.37 us -> 0.93 us
  transfers between devices with their start and end apart: 7 -> 7, of which waited for: 3 -> 3; matrix products, arithmetic and copies ran while one was open for 0% -> 0% of each run, Pallas kernels for 16% -> 14%
where the time goes in v2:
time: 51.7 us; the launch traced here: 51.6 us
  starting transfers between devices  33.9 us (66%)
  Pallas kernels  9.3 us (18%)
  waiting for transfers between devices  7.43 us (14%)
  local copies, waits for them, and re-layouts  0.93 us (2%)
    ppermute x6, starting transfers between devices, swap(): return lax.ppermute(value, AXES, pairs)  18.2 us
    all_to_all x1, starting transfers between devices, per_device(): everyone = lax.all_to_all(fastest, AXES, 0, 0, tiled=True)  15.6 us
    ppermute x6, waiting for transfers between devices, swap(): return lax.ppermute(value, AXES, pairs)  7.43 us
    pallas_call x1, Pallas kernels, per_device(): call(change_kernel, [(2, rows, LANES), half, half], 2 * 10 ** 7)  7.16 us
    pallas_call x1, Pallas kernels, per_device(): call(place_kernel, [(FIELDS, CAP, TILES * LANES)], 10 ** 6, [pltpu.VMEM((...  1.22 us
  transfers between devices with their start and end apart: 7, of which 3 were waited for; matrix products, arithmetic and copies ran while one was open for 0% of the time, Pallas kernels for 14%

profile of v2, /device:TPU:1, one launch (start us, length us, event | category | flops | bytes accessed | tf_op | source)
XLA Modules:
  0.0 51.6 jit_solution(4632397122660483978)
XLA Ops:
  0.0 0.0 copy-start
  0.0 0.9 %copy-done = f32[8,12,512]{2,0,1:T(8,128)S(1)} copy-done((f32[8,12,512]{2,0,1:T(8,128)S(1)}, f32[8,12,512]{2,0,1:T(8,128)}, u32[]{:S(2)}) %copy-start) | copy-done | bytes 196632
  0.9 0.0 copy-start.1
  0.9 0.9 %shard_map.28 = (f32[96,128]{1,0:T(8,128)S(1)}, f32[96,128]{1,0:T(8,128)S(1)}, f32[96,128]{1,0:T(8,128)S(1)}, f32[96,128]{1,0:T(8,128)S(1)}, f32[256,128]{1,0:T(8,128)}) custom-call(f32[384,128]{1,0:T(8,128)S(1)} %bitcast.10), custom_call_target="tpu_custom_call" | custom-call | flops 1000000 | bytes 125000 | tf_op jit(solution)/shard_map/pallas_call | solution.py:286
  1.8 15.6 %all-to-all-start = ((f32[256,1,128]{2,1,0:T(1,128)}), f32[256,1,128]{2,1,0:T(1,128)S(1)}, u32[]{:S(2)}, u32[]{:S(2)}) async-start(f32[256,1,128]{2,1,0:T(1,128)} %bitcast.4), calls=%async_computation | async-start | bytes 262144 | tf_op jit(solution)/shard_map/all_to_all | solution.py:289
  17.5 2.7 %collective-permute-start = (f32[96,128]{1,0:T(8,128)S(1)}, f32[96,128]{1,0:T(8,128)S(1)}, u32[]{:S(2)}, u32[]{:S(2)}) collective-permute-start(f32[96,128]{1,0:T(8,128)S(1)} %get-tuple-element.14), channel_id=1, source_target_pairs={{0,16},{1,17},{2,18},{3,19},{4,20},{5,21},{6,22},{7,23},{8,24},{9,... | collective-permute-start | bytes 147464 | tf_op jit(solution)/shard_map/ppermute | solution.py:277
  20.2 6.0 %collective-permute-start.1 = (f32[96,128]{1,0:T(8,128)S(1)}, f32[96,128]{1,0:T(8,128)S(1)}, u32[]{:S(2)}, u32[]{:S(2)}) collective-permute-start(f32[96,128]{1,0:T(8,128)S(1)} %get-tuple-element.15), channel_id=1, source_target_pairs={{0,240},{1,241},{2,242},{3,243},{4,244},{5,245},{6,246},{7,247},{8... | collective-permute-start | bytes 147464 | tf_op jit(solution)/shard_map/ppermute | solution.py:277
  26.2 0.9 %collective-permute-start.2 = (f32[96,128]{1,0:T(8,128)S(1)}, f32[96,128]{1,0:T(8,128)S(1)}, u32[]{:S(2)}, u32[]{:S(2)}) collective-permute-start(f32[96,128]{1,0:T(8,128)S(1)} %get-tuple-element.16), channel_id=1, source_target_pairs={{0,1},{1,0},{2,3},{3,2},{4,5},{5,4},{6,7},{7,6},{8,9},{9,8},{10,11... | collective-permute-start | bytes 147464 | tf_op jit(solution)/shard_map/ppermute | solution.py:277
  27.2 1.1 %collective-permute-start.3 = (f32[96,128]{1,0:T(8,128)S(1)}, f32[96,128]{1,0:T(8,128)S(1)}, u32[]{:S(2)}, u32[]{:S(2)}) collective-permute-start(f32[96,128]{1,0:T(8,128)S(1)} %get-tuple-element.17), channel_id=1, source_target_pairs={{0,255},{1,2},{2,1},{3,4},{4,3},{5,6},{6,5},{7,8},{8,7},{9,10},{10... | collective-permute-start | bytes 147464 | tf_op jit(solution)/shard_map/ppermute | solution.py:277
  28.3 0.0 collective-permute-done.x_first_ref
  28.3 0.2 collective-permute-done.1.x_second_ref
  28.5 0.0 collective-permute-done.2.y_inner_ref
  28.5 2.2 %collective-permute-done.3.y_outer_ref = f32[96,128]{1,0:T(8,128)S(1)} collective-permute-done((f32[96,128]{1,0:T(8,128)S(1)}, f32[96,128]{1,0:T(8,128)S(1)}, u32[]{:S(2)}, u32[]{:S(2)}) %collective-permute-start.3) | collective-permute-done | bytes 49184 | tf_op jit(solution)/shard_map/ppermute | solution.py:277
  30.7 0.0 copy-done.1
  30.7 0.0 copy-start.2
  30.7 7.2 %shard_map.29 = (f32[2,384,128]{2,1,0:T(8,128)S(1)}, f32[2,192,128]{2,1,0:T(8,128)S(1)}, f32[2,192,128]{2,1,0:T(8,128)S(1)}) custom-call(f32[384,128]{1,0:T(8,128)S(1)} %bitcast.11, f32[96,128]{1,0:T(8,128)S(1)} %collective-permute-done.x_first_ref, f32[96,128]{1,0:T(8,128)S(1)} %collective-permute-done.1.x_second_ref, ...), custom_call_target="tpu_custom_call" | custom-call | flops 20000000 | bytes 2500000 | tf_op jit(solution)/shard_map/pallas_call | solution.py:299
  37.9 5.5 %collective-permute-start.4 = (f32[2,192,128]{2,1,0:T(8,128)S(1)}, f32[2,192,128]{2,1,0:T(8,128)S(1)}, u32[]{:S(2)}, u32[]{:S(2)}) collective-permute-start(f32[2,192,128]{2,1,0:T(8,128)S(1)} %get-tuple-element.19), channel_id=1, source_target_pairs={{0,1},{1,0},{2,3},{3,2},{4,5},{5,4},{6,7},{7,6},{8,9},{9,8},{10,11... | collective-permute-start | bytes 589832 | tf_op jit(solution)/shard_map/ppermute | solution.py:277
  43.4 1.9 %collective-permute-start.5 = (f32[2,192,128]{2,1,0:T(8,128)S(1)}, f32[2,192,128]{2,1,0:T(8,128)S(1)}, u32[]{:S(2)}, u32[]{:S(2)}) collective-permute-start(f32[2,192,128]{2,1,0:T(8,128)S(1)} %get-tuple-element.20), channel_id=1, source_target_pairs={{1,2},{2,1},{3,4},{4,3},{5,6},{6,5},{7,8},{8,7},{9,10},{10,9},{11,... | collective-permute-start | bytes 589832 | tf_op jit(solution)/shard_map/ppermute | solution.py:277
  45.3 0.0 collective-permute-done.4.inner_ref
  45.3 5.0 %collective-permute-done.5.outer_ref = f32[2,192,128]{2,1,0:T(8,128)S(1)} collective-permute-done((f32[2,192,128]{2,1,0:T(8,128)S(1)}, f32[2,192,128]{2,1,0:T(8,128)S(1)}, u32[]{:S(2)}, u32[]{:S(2)}) %collective-permute-start.5) | collective-permute-done | bytes 196640 | tf_op jit(solution)/shard_map/ppermute | solution.py:277
  50.4 0.0 all-to-all-done
  50.4 0.0 copy-done.2
  50.4 1.2 %shard_map.30 = f32[8,24,512]{2,1,0:T(8,128)} custom-call(f32[256,128]{1,0:T(8,128)S(1)} %bitcast.12, f32[2,384,128]{2,1,0:T(8,128)S(1)} %get-tuple-element.18.own_ref, f32[2,192,128]{2,1,0:T(8,128)S(1)} %collective-permute-done.4.inner_ref, f32[2,192,128]{2,1,0:T(8,128)S(1)} %collective-permute-done.5.outer_ref, s32[24,128]{1,0:T(8,128)S(1)} %bitcast.13), custom_call_target="tpu_custom_call" | custom-call | flops 1000000 | bytes 125000 | tf_op jit(solution)/shard_map/pallas_call | solution.py:304
Async XLA Ops:
  0.0 0.9 %copy-start = (f32[8,12,512]{2,0,1:T(8,128)S(1)}, f32[8,12,512]{2,0,1:T(8,128)}, u32[]{:S(2)}) copy-start(f32[8,12,512]{2,0,1:T(8,128)} %param.3) | copy-start | bytes 589828
  0.9 29.8 %copy-start.1 = (f32[8,12,512]{2,0,1:T(8,128)S(1)}, f32[8,12,512]{2,0,1:T(8,128)}, u32[]{:S(2)}) copy-start(f32[8,12,512]{2,0,1:T(8,128)} %param.3) | copy-start | bytes 589828
  1.8 48.5 %all-to-all-start = ((f32[256,1,128]{2,1,0:T(1,128)}), f32[256,1,128]{2,1,0:T(1,128)S(1)}, u32[]{:S(2)}, u32[]{:S(2)}) async-start(f32[256,1,128]{2,1,0:T(1,128)} %bitcast.4), calls=%async_computation | async-start | bytes 262144 | tf_op jit(solution)/shard_map/all_to_all | solution.py:289
  17.5 10.8 %collective-permute-start = (f32[96,128]{1,0:T(8,128)S(1)}, f32[96,128]{1,0:T(8,128)S(1)}, u32[]{:S(2)}, u32[]{:S(2)}) collective-permute-start(f32[96,128]{1,0:T(8,128)S(1)} %get-tuple-element.14), channel_id=1, source_target_pairs={{0,16},{1,17},{2,18},{3,19},{4,20},{5,21},{6,22},{7,23},{8,24},{9,... | collective-permute-start | bytes 147464 | tf_op jit(solution)/shard_map/ppermute | solution.py:277
  20.2 8.3 %collective-permute-start.1 = (f32[96,128]{1,0:T(8,128)S(1)}, f32[96,128]{1,0:T(8,128)S(1)}, u32[]{:S(2)}, u32[]{:S(2)}) collective-permute-start(f32[96,128]{1,0:T(8,128)S(1)} %get-tuple-element.15), channel_id=1, source_target_pairs={{0,240},{1,241},{2,242},{3,243},{4,244},{5,245},{6,246},{7,247},{8... | collective-permute-start | bytes 147464 | tf_op jit(solution)/shard_map/ppermute | solution.py:277
  26.2 2.3 %collective-permute-start.2 = (f32[96,128]{1,0:T(8,128)S(1)}, f32[96,128]{1,0:T(8,128)S(1)}, u32[]{:S(2)}, u32[]{:S(2)}) collective-permute-start(f32[96,128]{1,0:T(8,128)S(1)} %get-tuple-element.16), channel_id=1, source_target_pairs={{0,1},{1,0},{2,3},{3,2},{4,5},{5,4},{6,7},{7,6},{8,9},{9,8},{10,11... | collective-permute-start | bytes 147464 | tf_op jit(solution)/shard_map/ppermute | solution.py:277
  27.2 3.5 %collective-permute-start.3 = (f32[96,128]{1,0:T(8,128)S(1)}, f32[96,128]{1,0:T(8,128)S(1)}, u32[]{:S(2)}, u32[]{:S(2)}) collective-permute-start(f32[96,128]{1,0:T(8,128)S(1)} %get-tuple-element.17), channel_id=1, source_target_pairs={{0,255},{1,2},{2,1},{3,4},{4,3},{5,6},{6,5},{7,8},{8,7},{9,10},{10... | collective-permute-start | bytes 147464 | tf_op jit(solution)/shard_map/ppermute | solution.py:277
  30.7 19.7 %copy-start.2 = (s32[3072]{0:T(1024)S(1)}, s32[3072]{0:T(1024)}, u32[]{:S(2)}) copy-start(s32[3072]{0:T(1024)} %param.4) | copy-start | bytes 36868
  37.9 7.4 %collective-permute-start.4 = (f32[2,192,128]{2,1,0:T(8,128)S(1)}, f32[2,192,128]{2,1,0:T(8,128)S(1)}, u32[]{:S(2)}, u32[]{:S(2)}) collective-permute-start(f32[2,192,128]{2,1,0:T(8,128)S(1)} %get-tuple-element.19), channel_id=1, source_target_pairs={{0,1},{1,0},{2,3},{3,2},{4,5},{5,4},{6,7},{7,6},{8,9},{9,8},{10,11... | collective-permute-start | bytes 589832 | tf_op jit(solution)/shard_map/ppermute | solution.py:277
  43.4 7.0 %collective-permute-start.5 = (f32[2,192,128]{2,1,0:T(8,128)S(1)}, f32[2,192,128]{2,1,0:T(8,128)S(1)}, u32[]{:S(2)}, u32[]{:S(2)}) collective-permute-start(f32[2,192,128]{2,1,0:T(8,128)S(1)} %get-tuple-element.20), channel_id=1, source_target_pairs={{1,2},{2,1},{3,4},{4,3},{5,6},{6,5},{7,8},{8,7},{9,10},{10,9},{11,... | collective-permute-start | bytes 589832 | tf_op jit(solution)/shard_map/ppermute | solution.py:277

commit v3 on v2

v3 whole, which is shorter than its diff:
```python
import functools

import jax
import jax.numpy as jnp
from jax import lax
from jax.experimental import pallas as pl
from jax.experimental.pallas import tpu as pltpu
from jax.sharding import PartitionSpec as P


BE = 8
GY = 16
AXES = ("outer", "inner")
GAMMA = 5.0 / 3.0
COURANT = 0.8
LANES = 128
TILES = 4
FIELDS = 8
BLOCKS = 12
REACH = 6
CAP = 24
ROWS = 16
HELD = 40
SIDE = FIELDS * 2 * BE
PITCH = BE + 2


def roll(value, shift):
    return pltpu.roll(value, shift % LANES, 1)


def half_minmod(former, latter):
    return 0.5 * (
        jnp.maximum(jnp.minimum(former, latter), 0.0)
        + jnp.minimum(jnp.maximum(former, latter), 0.0)
    )


def sound(density, pressure, field_sq):
    pushed = GAMMA * pressure + field_sq
    return pushed * lax.rsqrt(pushed * density)


def squared(state):
    return state[5] * state[5] + state[6] * state[6] + state[7] * state[7]


def conserved(state, field_sq):
    density, pressure = state[0], state[4]
    momentum = [density * state[1 + k] for k in range(3)]
    kinetic = momentum[0] * state[1] + momentum[1] * state[2] + momentum[2] * state[3]
    energy = pressure * (1.0 / (GAMMA - 1.0)) + 0.5 * (kinetic + field_sq)
    return [density, *momentum, energy, state[5], state[6], state[7]]


def flux_parts(state, normal):
    field_sq = squared(state)
    total_pressure = state[4] + 0.5 * field_sq
    whole = conserved(state, field_sq)
    speed, field = state[1 + normal], state[5 + normal]
    along = state[1] * state[5] + state[2] * state[6] + state[3] * state[7]
    momentum = [whole[1 + k] * speed - state[5 + k] * field for k in range(3)]
    momentum[normal] = momentum[normal] + total_pressure
    induction = [
        None if k == normal else state[5 + k] * speed - state[1 + k] * field for k in range(3)
    ]
    energy = (whole[4] + total_pressure) * speed - field * along
    signal = jnp.abs(speed) + sound(state[0], state[4], field_sq)
    return [whole[1 + normal], *momentum, energy, *induction], signal, whole


def twice_face_flux(left, right, normal):
    flux_left, signal_left, whole_left = flux_parts(left, normal)
    flux_right, signal_right, whole_right = flux_parts(right, normal)
    fastest = jnp.maximum(signal_left, signal_right)
    result = []
    for k in range(FIELDS):
        spread = fastest * (whole_right[k] - whole_left[k])
        result.append(-spread if flux_left[k] is None else flux_left[k] + flux_right[k] - spread)
    return result


def rows_of(index):
    return slice(index * ROWS, (index + 1) * ROWS)


def device_index():
    return lax.axis_index(AXES[0]) * lax.axis_size(AXES[1]) + lax.axis_index(AXES[1])


def turn(first, second):
    row = lax.broadcasted_iota(jnp.int32, (8, LANES), 0)
    lane = lax.broadcasted_iota(jnp.int32, (8, LANES), 1)
    group, place = lane // 8, lane % 8

    def along(value, source):
        return jnp.take_along_axis(value, source, axis=1, mode="promise_in_bounds")

    def across(index):
        source = (group - row - index) % 16
        picked = [
            jnp.take_along_axis(value, source % 8, axis=0, mode="promise_in_bounds")
            for value in (first, second)
        ]
        return jnp.where(source < 8, picked[0], picked[1])

    first = along(first, (group - row) % 16 * 8 + place)
    second = along(second, (group - row - 8) % 16 * 8 + place)
    upper, lower = across(0), across(8)
    return (
        along(upper, (group + row) % 16 * 8 + place),
        along(lower, (group + row + 8) % 16 * 8 + place),
    )


def prepare_kernel(
    prim_ref, x_first_ref, x_second_ref, y_inner_ref, y_outer_ref, fastest_ref, cells_ref, whole_ref
):
    device = device_index()
    odd_row = (device // GY) % 2 == 1
    odd = device % 2 == 1
    cells = []
    for k in range(FIELDS):
        line = []
        for tile in range(TILES):
            part = prim_ref[pl.ds(tile * FIELDS + k, BLOCKS, stride=TILES * FIELDS)]
            line.append(jnp.concatenate([part, part[:1], part[:2], part[-1:]], 0))
        cells.append(line)
    best = None
    for tile in range(TILES):
        state = [cells[k][tile] for k in range(FIELDS)]
        field_sq = squared(state)
        speed = (
            jnp.abs(state[1])
            + jnp.abs(state[2])
            + jnp.abs(state[3])
            + 3.0 * sound(state[0], state[4], field_sq)
        )
        best = speed if best is None else jnp.maximum(best, speed)
        for k, value in enumerate(conserved(state, field_sq)):
            whole_ref[rows_of(k * TILES + tile)] = value
    fastest_ref[...] = jnp.broadcast_to(jnp.max(best, keepdims=True), fastest_ref.shape)
    for k in range(FIELDS):
        for tile in range(TILES):
            halves = turn(cells[k][tile][:8], cells[k][tile][8:])
            base = (k * BE + 2 * tile) * BE
            cells_ref[base : base + 8], cells_ref[base + 8 : base + 16] = halves
    to_first = jnp.where(odd_row, 0, BE - 2)
    to_second = jnp.where(odd_row, BE - 2, 0)
    to_inner = jnp.where(odd, 0, BE - 2)
    to_outer = jnp.where(odd, BE - 2, 0)
    for k in range(FIELDS):
        base, there = k * BE * BE, slice(k * 2 * BE, (k + 1) * 2 * BE)
        for start, ref in ((to_first, x_first_ref), (to_second, x_second_ref)):
            ref[there] = cells_ref[pl.ds(pl.multiple_of(base + start * BE, BE), 2 * BE)]
        for start, ref in ((to_inner, y_inner_ref), (to_outer, y_outer_ref)):
            for layer in range(2):
                row = (2 * k + layer) * BE
                ref[row : row + BE] = cells_ref[pl.ds(base + start + layer, BE, stride=BE)]
    send_half(whole_ref, y_inner_ref, y_outer_ref, SIDE, odd)


def send_half(source, inner_ref, outer_ref, base, odd):
    to_inner = jnp.where(odd, 0, REACH)
    to_outer = jnp.where(odd, REACH, 0)
    for row in range(FIELDS * TILES):
        there = slice(base + row * REACH, base + (row + 1) * REACH)
        inner_ref[there] = source[pl.ds(row * ROWS + to_inner, REACH)]
        outer_ref[there] = source[pl.ds(row * ROWS + to_outer, REACH)]


def change_kernel(
    cells_ref,
    x_first_ref,
    x_second_ref,
    y_inner_ref,
    y_outer_ref,
    own_ref,
    inner_ref,
    outer_ref,
    line_ref,
    right_ref,
    face_ref,
):
    device = device_index()
    odd_row = (device // GY) % 2 == 1
    odd = device % 2 == 1
    fields = range(FIELDS)

    def cell(x, k):
        return cells_ref[(k * BE + x) * BE : (k * BE + x + 1) * BE]

    def halo(first, second, k, layer, flag):
        rows = slice((2 * k + layer) * BE, (2 * k + layer + 1) * BE)
        return jnp.where(flag, first[rows], second[rows])

    def padded(x, k, y):
        return slice((k * BE + x) * PITCH + y + 1, (k * BE + x) * PITCH + y + 1 + BE)

    def all_x(k, y):
        return pl.ds(k * BE * PITCH + y + 1, BE, stride=PITCH)

    def column(x):
        if x < 0:
            return [halo(x_first_ref, x_second_ref, k, x + 2, odd_row) for k in fields]
        if x >= BE:
            return [halo(x_second_ref, x_first_ref, k, x - BE, odd_row) for k in fields]
        return [cell(x, k) for k in fields]

    total = [None] * BE
    here, up = column(-2), column(-1)
    ahead = [up[k] - here[k] for k in fields]
    left = last_face = None
    for x in range(-1, BE + 1):
        here, up, behind = up, column(x + 1), ahead
        ahead = [up[k] - here[k] for k in fields]
        half = [half_minmod(behind[k], ahead[k]) for k in fields]
        if left is not None:
            face = twice_face_flux(left, [here[k] - half[k] for k in fields], 0)
            if last_face is not None:
                total[x - 1] = [face[k] - last_face[k] for k in fields]
            last_face = face
        left = [here[k] + half[k] for k in fields]

    low_left, low_right = [], []
    for k in fields:
        far = halo(y_inner_ref, y_outer_ref, k, 0, odd)
        near = halo(y_inner_ref, y_outer_ref, k, 1, odd)
        edge = cells_ref[pl.ds(k * BE * BE, BE, stride=BE)]
        after = cells_ref[pl.ds(k * BE * BE + 1, BE, stride=BE)]
        low_left.append(near + half_minmod(near - far, edge - near))
        low_right.append(edge - half_minmod(edge - near, after - edge))
        line_ref[all_x(k, -1)] = near
        near = halo(y_outer_ref, y_inner_ref, k, 0, odd)
        far = halo(y_outer_ref, y_inner_ref, k, 1, odd)
        edge = cells_ref[pl.ds(k * BE * BE + BE - 1, BE, stride=BE)]
        line_ref[all_x(k, BE)] = near
        right_ref[all_x(k, BE)] = near - half_minmod(near - edge, far - near)
    for k, value in enumerate(twice_face_flux(low_left, low_right, 1)):
        face_ref[all_x(k, -1)] = value
    for x in range(BE):
        for k in fields:
            line_ref[padded(x, k, 0)] = cell(x, k)
    for x in range(BE):
        state = [cell(x, k) for k in fields]
        left = []
        for k in fields:
            half = half_minmod(
                state[k] - line_ref[padded(x, k, -1)], line_ref[padded(x, k, 1)] - state[k]
            )
            left.append(state[k] + half)
            right_ref[padded(x, k, 0)] = state[k] - half
        face = twice_face_flux(left, [right_ref[padded(x, k, 1)] for k in fields], 1)
        for k in fields:
            face_ref[padded(x, k, 0)] = face[k]
        for k in fields:
            total[x][k] = total[x][k] + (face[k] - face_ref[padded(x, k, -1)])

        left, right = [], []
        for k in fields:
            ahead = roll(state[k], -1) - state[k]
            half = half_minmod(roll(ahead, 1), ahead)
            left.append(state[k] + half)
            right.append(roll(state[k] - half, -1))
        face = twice_face_flux(left, right, 2)
        for k in fields:
            total[x][k] = total[x][k] + (face[k] - roll(face[k], 1))

    for k in fields:
        for tile in range(TILES):
            base = (k * TILES + tile) * ROWS
            halves = turn(total[2 * tile][k], total[2 * tile + 1][k])
            own_ref[base : base + 8], own_ref[base + 8 : base + 16] = halves
    send_half(own_ref, inner_ref, outer_ref, 0, odd)


def place_kernel(
    fastest_ref,
    whole_ref,
    change_ref,
    whole_inner_ref,
    whole_outer_ref,
    inner_ref,
    outer_ref,
    owner_ref,
    out_ref,
    held_ref,
):
    device = device_index()
    odd = device % 2 == 1
    owners = owner_ref[...]
    first = jnp.sum((owners < device).astype(jnp.int32)) - (device * BLOCKS - REACH)
    count = jnp.sum((owners == device).astype(jnp.int32))
    first = jnp.clip(first, 0, BLOCKS) + 2
    scale = (0.5 * COURANT) / jnp.max(fastest_ref[...])
    live = lax.broadcasted_iota(jnp.int32, (CAP, LANES), 0) < count
    for row in range(FIELDS * TILES):
        there = slice(row * REACH, (row + 1) * REACH)
        sent = slice(SIDE + row * REACH, SIDE + (row + 1) * REACH)
        inner = whole_inner_ref[sent] - scale * inner_ref[there]
        outer = whole_outer_ref[sent] - scale * outer_ref[there]
        base = row * HELD
        held_ref[base + 8 : base + 8 + ROWS] = (
            whole_ref[rows_of(row)] - scale * change_ref[rows_of(row)]
        )
        held_ref[base + 2 : base + 8] = jnp.where(odd, inner, outer)
        held_ref[base + 20 : base + 26] = jnp.where(odd, outer, inner)
    for row in range(FIELDS * TILES):
        k, tile = divmod(row, TILES)
        value = held_ref[pl.ds(row * HELD + first, CAP)]
        out_ref[k, :, tile * LANES : (tile + 1) * LANES] = jnp.where(live, value, 0.0)


def call(kernel, outs, flops, scratch=()):
    return pl.pallas_call(
        kernel,
        out_shape=[
            jax.ShapeDtypeStruct(out if isinstance(out, tuple) else (out, LANES), jnp.float32)
            for out in outs
        ],
        scratch_shapes=list(scratch),
        cost_estimate=pl.CostEstimate(flops=flops, bytes_accessed=flops // 8, transcendentals=0),
        compiler_params=pltpu.CompilerParams(vmem_limit_bytes=8 * 2**20),
    )


def swap(value, partner, devices):
    pairs = [(i, partner(i) % devices) for i in range(devices) if partner(i) is not None]
    return lax.ppermute(value, AXES, pairs)


def per_device(ranks, prim, new_owner, new_slot):
    del new_slot
    devices = lax.axis_size(AXES)
    raw = prim.reshape(FIELDS, BLOCKS, TILES, LANES).transpose(1, 2, 0, 3).reshape(-1, LANES)
    half = FIELDS * TILES * REACH
    whole = FIELDS * TILES * ROWS
    x_first, x_second, y_inner, y_outer, fastest, cells, conserved_own = call(
        prepare_kernel,
        [SIDE, SIDE, SIDE + half, SIDE + half, devices, FIELDS * BE * BE, whole],
        10**6,
    )(raw)
    everyone = lax.all_to_all(fastest, AXES, 0, 0, tiled=True)

    def within(i, j):
        return j if 0 <= j < devices and i // ranks == j // ranks else None

    x_first = swap(x_first, lambda i: i + GY if (i // GY) % 2 == 0 else i - GY, devices)
    x_second = swap(x_second, lambda i: i + GY if (i // GY) % 2 == 1 else i - GY, devices)
    y_outer = swap(y_outer, lambda i: i + 1 if i % 2 == 1 else i - 1, devices)
    y_inner = swap(y_inner, lambda i: i ^ 1, devices)
    padded = pltpu.VMEM((FIELDS * BE * PITCH, LANES), jnp.float32)
    own, to_inner, to_outer = call(
        change_kernel, [whole, half, half], 2 * 10**7, [padded, padded, padded]
    )(cells, x_first, x_second, y_inner, y_outer)
    from_outer = swap(to_outer, lambda i: within(i, i + 1 if i % 2 == 1 else i - 1), devices)
    from_inner = swap(to_inner, lambda i: i ^ 1, devices)
    (placed,) = call(
        place_kernel,
        [(FIELDS, CAP, TILES * LANES)],
        10**6,
        [pltpu.VMEM((FIELDS * TILES * HELD, LANES), jnp.float32)],
    )(everyone, conserved_own, own, y_inner, y_outer, from_inner, from_outer, new_owner.reshape(-1, LANES))
    return placed


def solution(mesh):
    return jax.shard_map(
        functools.partial(per_device, mesh.shape["inner"]),
        mesh=mesh,
        in_specs=(P(None, AXES, None), P(), P()),
        out_specs=P(None, AXES, None),
        check_vma=False,
    )
```

time: 51.7 us -> 44.6 us (0.86)
  the two profiles are of different devices: /device:TPU:1 before, /device:TPU:57 now
where the time goes in v3:
time: 44.6 us; the launch traced here: 44.4 us
  starting transfers between devices  26.7 us (60%)
  waiting for transfers between devices  10.5 us (24%)
  Pallas kernels  6.25 us (14%)
  local copies, waits for them, and re-layouts  0.93 us (2%)
    all_to_all x1, starting transfers between devices, per_device(): everyone = lax.all_to_all(fastest, AXES, 0, 0, tiled=True)  14.3 us
    ppermute x6, starting transfers between devices, swap(): return lax.ppermute(value, AXES, pairs)  12.4 us
    ppermute x6, waiting for transfers between devices, swap(): return lax.ppermute(value, AXES, pairs)  10.5 us
    pallas_call x1, Pallas kernels, per_device(): call(change_kernel, [whole, half, half], 2 * 10 ** 7, [padded, padded, pa...  3.79 us
    pallas_call x1, Pallas kernels, per_device(): call(prepare_kernel, [SIDE, SIDE, SIDE + half, SIDE + half, devices, FIEL...  1.46 us
    pallas_call x1, Pallas kernels, per_device(): call(place_kernel, [(FIELDS, CAP, TILES * LANES)], 10 ** 6, [pltpu.VMEM((...  1 us
    unnamed x4, local copies, waits for them, and re-layouts  0.93 us
  transfers between devices with their start and end apart: 7, of which 2 were waited for; matrix products, arithmetic and copies ran while one was open for 0% of the time, Pallas kernels for 9%

profile of v3, /device:TPU:57, one launch (start us, length us, event | category | flops | bytes accessed | tf_op | source)
XLA Modules:
  0.0 44.4 jit_solution(14199037127460899768)
XLA Ops:
  0.0 0.0 copy-start
  0.0 0.9 %copy-done = f32[8,12,512]{2,0,1:T(8,128)S(1)} copy-done((f32[8,12,512]{2,0,1:T(8,128)S(1)}, f32[8,12,512]{2,0,1:T(8,128)}, u32[]{:S(2)}) %copy-start) | copy-done | bytes 196632
  0.9 1.5 %shard_map.28 = (f32[128,128]{1,0:T(8,128)S(1)}, f32[128,128]{1,0:T(8,128)S(1)}, f32[320,128]{1,0:T(8,128)S(1)}, f32[320,128]{1,0:T(8,128)S(1)}, f32[256,128]{1,...) custom-call(f32[384,128]{1,0:T(8,128)S(1)} %bitcast.11), custom_call_target="tpu_custom_call" | custom-call | flops 1000000 | bytes 125000 | tf_op jit(solution)/shard_map/pallas_call | solution.py:338
  2.4 0.7 %collective-permute-start.2 = (f32[320,128]{1,0:T(8,128)S(1)}, f32[320,128]{1,0:T(8,128)S(1)}, u32[]{:S(2)}, u32[]{:S(2)}) collective-permute-start(f32[320,128]{1,0:T(8,128)S(1)} %get-tuple-element.20), channel_id=1, source_target_pairs={{0,1},{1,0},{2,3},{3,2},{4,5},{5,4},{6,7},{7,6},{8,9},{9,8},{10,11... | collective-permute-start | bytes 491528 | tf_op jit(solution)/shard_map/ppermute | solution.py:329
  3.1 1.2 %collective-permute-start.3 = (f32[320,128]{1,0:T(8,128)S(1)}, f32[320,128]{1,0:T(8,128)S(1)}, u32[]{:S(2)}, u32[]{:S(2)}) collective-permute-start(f32[320,128]{1,0:T(8,128)S(1)} %get-tuple-element.21), channel_id=1, source_target_pairs={{0,255},{1,2},{2,1},{3,4},{4,3},{5,6},{6,5},{7,8},{8,7},{9,10},{10... | collective-permute-start | bytes 491528 | tf_op jit(solution)/shard_map/ppermute | solution.py:329
  4.2 14.3 %all-to-all-start = ((f32[256,1,128]{2,1,0:T(1,128)}), f32[256,1,128]{2,1,0:T(1,128)S(1)}, u32[]{:S(2)}, u32[]{:S(2)}) async-start(f32[256,1,128]{2,1,0:T(1,128)} %bitcast.4), calls=%async_computation | async-start | bytes 262144 | tf_op jit(solution)/shard_map/all_to_all | solution.py:343
  18.5 2.7 %collective-permute-start = (f32[128,128]{1,0:T(8,128)S(1)}, f32[128,128]{1,0:T(8,128)S(1)}, u32[]{:S(2)}, u32[]{:S(2)}) collective-permute-start(f32[128,128]{1,0:T(8,128)S(1)} %get-tuple-element.18), channel_id=1, source_target_pairs={{0,16},{1,17},{2,18},{3,19},{4,20},{5,21},{6,22},{7,23},{8,24},{9,... | collective-permute-start | bytes 196616 | tf_op jit(solution)/shard_map/ppermute | solution.py:329
  21.2 5.1 %collective-permute-start.1 = (f32[128,128]{1,0:T(8,128)S(1)}, f32[128,128]{1,0:T(8,128)S(1)}, u32[]{:S(2)}, u32[]{:S(2)}) collective-permute-start(f32[128,128]{1,0:T(8,128)S(1)} %get-tuple-element.19), channel_id=1, source_target_pairs={{0,240},{1,241},{2,242},{3,243},{4,244},{5,245},{6,246},{7,247},{8... | collective-permute-start | bytes 196616 | tf_op jit(solution)/shard_map/ppermute | solution.py:329
  26.3 0.0 collective-permute-done.x_first_ref
  26.3 4.4 %collective-permute-done.1.x_second_ref = f32[128,128]{1,0:T(8,128)S(1)} collective-permute-done((f32[128,128]{1,0:T(8,128)S(1)}, f32[128,128]{1,0:T(8,128)S(1)}, u32[]{:S(2)}, u32[]{:S(2)}) %collective-permute-start.1) | collective-permute-done | bytes 65568 | tf_op jit(solution)/shard_map/ppermute | solution.py:329
  30.7 0.0 collective-permute-done.2.y_inner_ref.whole_inner_ref
  30.7 0.0 collective-permute-done.3.y_outer_ref.whole_outer_ref
  30.7 0.0 copy-start.1
  30.7 3.8 %shard_map.29 = (f32[512,128]{1,0:T(8,128)S(1)}, f32[192,128]{1,0:T(8,128)S(1)}, f32[192,128]{1,0:T(8,128)S(1)}) custom-call(f32[512,128]{1,0:T(8,128)S(1)} %get-tuple-element.17.cells_ref, f32[128,128]{1,0:T(8,128)S(1)} %collective-permute-done.x_first_ref, f32[128,128]{1,0:T(8,128)S(1)} %collective-permute-done.1.x_second_ref, ...), custom_call_target="tpu_custom_call" | custom-call | flops 20000000 | bytes 2500000 | tf_op jit(solution)/shard_map/pallas_call | solution.py:353
  34.5 0.8 %collective-permute-start.4 = (f32[192,128]{1,0:T(8,128)S(1)}, f32[192,128]{1,0:T(8,128)S(1)}, u32[]{:S(2)}, u32[]{:S(2)}) collective-permute-start(f32[192,128]{1,0:T(8,128)S(1)} %get-tuple-element.23), channel_id=1, source_target_pairs={{0,1},{1,0},{2,3},{3,2},{4,5},{5,4},{6,7},{7,6},{8,9},{9,8},{10,11... | collective-permute-start | bytes 294920 | tf_op jit(solution)/shard_map/ppermute | solution.py:329
  35.4 1.9 %collective-permute-start.5 = (f32[192,128]{1,0:T(8,128)S(1)}, f32[192,128]{1,0:T(8,128)S(1)}, u32[]{:S(2)}, u32[]{:S(2)}) collective-permute-start(f32[192,128]{1,0:T(8,128)S(1)} %get-tuple-element.24), channel_id=1, source_target_pairs={{1,2},{2,1},{3,4},{4,3},{5,6},{6,5},{7,8},{8,7},{9,10},{10,9},{11,... | collective-permute-start | bytes 294920 | tf_op jit(solution)/shard_map/ppermute | solution.py:329
  37.3 0.0 all-to-all-done
  37.3 0.0 collective-permute-done.4.inner_ref
  37.3 6.1 %collective-permute-done.5.outer_ref = f32[192,128]{1,0:T(8,128)S(1)} collective-permute-done((f32[192,128]{1,0:T(8,128)S(1)}, f32[192,128]{1,0:T(8,128)S(1)}, u32[]{:S(2)}, u32[]{:S(2)}) %collective-permute-start.5) | collective-permute-done | bytes 98336 | tf_op jit(solution)/shard_map/ppermute | solution.py:329
  43.4 0.0 copy-done.1
  43.4 1.0 %shard_map.30 = f32[8,24,512]{2,1,0:T(8,128)} custom-call(f32[256,128]{1,0:T(8,128)S(1)} %bitcast.10, f32[512,128]{1,0:T(8,128)S(1)} %get-tuple-element.16.whole_ref, f32[512,128]{1,0:T(8,128)S(1)} %get-tuple-element.22.change_ref, f32[320,128]{1,0:T(8,128)S(1)} %collective-permute-done.2.y_inner_ref.whole_inner_ref, ...), custom_call_target="tpu_custom_call" | custom-call | flops 1000000 | bytes 125000 | tf_op jit(solution)/shard_map/pallas_call | solution.py:358
Async XLA Ops:
  0.0 0.9 %copy-start = (f32[8,12,512]{2,0,1:T(8,128)S(1)}, f32[8,12,512]{2,0,1:T(8,128)}, u32[]{:S(2)}) copy-start(f32[8,12,512]{2,0,1:T(8,128)} %param.3) | copy-start | bytes 589828
  2.4 28.3 %collective-permute-start.2 = (f32[320,128]{1,0:T(8,128)S(1)}, f32[320,128]{1,0:T(8,128)S(1)}, u32[]{:S(2)}, u32[]{:S(2)}) collective-permute-start(f32[320,128]{1,0:T(8,128)S(1)} %get-tuple-element.20), channel_id=1, source_target_pairs={{0,1},{1,0},{2,3},{3,2},{4,5},{5,4},{6,7},{7,6},{8,9},{9,8},{10,11... | collective-permute-start | bytes 491528 | tf_op jit(solution)/shard_map/ppermute | solution.py:329
  3.1 27.7 %collective-permute-start.3 = (f32[320,128]{1,0:T(8,128)S(1)}, f32[320,128]{1,0:T(8,128)S(1)}, u32[]{:S(2)}, u32[]{:S(2)}) collective-permute-start(f32[320,128]{1,0:T(8,128)S(1)} %get-tuple-element.21), channel_id=1, source_target_pairs={{0,255},{1,2},{2,1},{3,4},{4,3},{5,6},{6,5},{7,8},{8,7},{9,10},{10... | collective-permute-start | bytes 491528 | tf_op jit(solution)/shard_map/ppermute | solution.py:329
  4.2 33.1 %all-to-all-start = ((f32[256,1,128]{2,1,0:T(1,128)}), f32[256,1,128]{2,1,0:T(1,128)S(1)}, u32[]{:S(2)}, u32[]{:S(2)}) async-start(f32[256,1,128]{2,1,0:T(1,128)} %bitcast.4), calls=%async_computation | async-start | bytes 262144 | tf_op jit(solution)/shard_map/all_to_all | solution.py:343
  18.5 7.8 %collective-permute-start = (f32[128,128]{1,0:T(8,128)S(1)}, f32[128,128]{1,0:T(8,128)S(1)}, u32[]{:S(2)}, u32[]{:S(2)}) collective-permute-start(f32[128,128]{1,0:T(8,128)S(1)} %get-tuple-element.18), channel_id=1, source_target_pairs={{0,16},{1,17},{2,18},{3,19},{4,20},{5,21},{6,22},{7,23},{8,24},{9,... | collective-permute-start | bytes 196616 | tf_op jit(solution)/shard_map/ppermute | solution.py:329
  21.2 9.5 %collective-permute-start.1 = (f32[128,128]{1,0:T(8,128)S(1)}, f32[128,128]{1,0:T(8,128)S(1)}, u32[]{:S(2)}, u32[]{:S(2)}) collective-permute-start(f32[128,128]{1,0:T(8,128)S(1)} %get-tuple-element.19), channel_id=1, source_target_pairs={{0,240},{1,241},{2,242},{3,243},{4,244},{5,245},{6,246},{7,247},{8... | collective-permute-start | bytes 196616 | tf_op jit(solution)/shard_map/ppermute | solution.py:329
  30.7 12.7 %copy-start.1 = (s32[3072]{0:T(1024)S(1)}, s32[3072]{0:T(1024)}, u32[]{:S(2)}) copy-start(s32[3072]{0:T(1024)} %param.4) | copy-start | bytes 36868
  34.5 2.8 %collective-permute-start.4 = (f32[192,128]{1,0:T(8,128)S(1)}, f32[192,128]{1,0:T(8,128)S(1)}, u32[]{:S(2)}, u32[]{:S(2)}) collective-permute-start(f32[192,128]{1,0:T(8,128)S(1)} %get-tuple-element.23), channel_id=1, source_target_pairs={{0,1},{1,0},{2,3},{3,2},{4,5},{5,4},{6,7},{7,6},{8,9},{9,8},{10,11... | collective-permute-start | bytes 294920 | tf_op jit(solution)/shard_map/ppermute | solution.py:329
  35.4 8.0 %collective-permute-start.5 = (f32[192,128]{1,0:T(8,128)S(1)}, f32[192,128]{1,0:T(8,128)S(1)}, u32[]{:S(2)}, u32[]{:S(2)}) collective-permute-start(f32[192,128]{1,0:T(8,128)S(1)} %get-tuple-element.24), channel_id=1, source_target_pairs={{1,2},{2,1},{3,4},{4,3},{5,6},{6,5},{7,8},{8,7},{9,10},{10,9},{11,... | collective-permute-start | bytes 294920 | tf_op jit(solution)/shard_map/ppermute | solution.py:329
